TPU v7x, 128 devices: a whole 4x4x4 slice. The times are simulated.
128 devices in a mesh: rep: 16 (over z_lo, y, core), tp: 8 (over z_hi, x).
Axes of the slice: x: 4, y: 4, z: 4 (z_hi: 2, z_lo: 2; z = z_hi * 2 + z_lo), core: 2. Of those that a mesh axis runs over, the one named last changes fastest.
Arguments:
- residual_in: bfloat16 [16, 512, 8192], P('rep', 'tp'), may hold values from -6 to 6
- norm_gain: bfloat16 [8192], replicated, may hold values from 0.099609375 to 1.8984375
- w_query: bfloat16 [8192, 4096], P(None, 'tp'), may hold values from -1 to 1
- w_keyval: bfloat16 [8192, 1024], P(None, 'tp'), may hold values from -0.0625 to 0.0625
- w_out: bfloat16 [4096, 8192], P('tp'), may hold values from -0.375 to 0.375
- score_head: bfloat16 [8192], replicated, may hold values from -0.0625 to 0.0625
- lengths: int32 [16], P('rep'), may hold values from 256 to 512
- policy_slots: bfloat16 [16, 768, 8192], P('rep', None, 'tp'), may hold values from -6 to 6
Outputs:
- scored_hidden: bfloat16 [16, 512, 8192], P('rep', 'tp')
- rewards: float32 [16], P('rep')
- policy_copies: bfloat16 [16, 768, 8192], P('rep', None, 'tp')
All inputs are finite; a program needn't handle non-finite values.
Results may differ from a plain program's by a relative error of at most 0.017.
The roundings to bfloat16 on the way count: a program that leaves them out, or rounds other values in their place, can miss the bound.
Values may be sent and summed in bfloat16 or wider, within the bound.
A program may use at most 128 MiB of HBM per device.

v0:
```python
import jax
import jax.numpy as jnp
from jax import lax
from jax.sharding import PartitionSpec as P

QH = 32
KVH = 4
HS = 128
KW = 512


def sent_to_all(value, axis):
    length = lax.axis_size(axis)
    return lax.all_to_all(
        jnp.broadcast_to(value[None], (length, *value.shape)), axis, 0, 0, tiled=True
    )


def joined_along(tiles, dim):
    shape = list(tiles.shape[1:])
    shape[dim] *= tiles.shape[0]
    return jnp.moveaxis(tiles, 0, dim).reshape(shape)


def collect(value, axis, dim):
    tiles = sent_to_all(value, axis)
    return joined_along(tiles, dim)


def taken_together(value, axis):
    return sent_to_all(value, axis).sum(axis=0)


def filled_up(lines, length):
    spare = -len(lines) % length
    return jnp.pad(lines, [(0, spare)] + [(0, 0)] * (lines.ndim - 1))


def spread(value, axis, root):
    lines = jnp.where(lax.axis_index(axis) == root, value, jnp.zeros_like(value)).reshape(
        -1, *value.shape[1:][-1:]
    )
    padded = filled_up(lines, lax.axis_size(axis))
    own = lax.psum_scatter(padded, axis, scatter_dimension=0, tiled=True)
    return lax.all_gather(own, axis, axis=0, tiled=True)[: len(lines)].reshape(value.shape)


def on_device(residual_in, norm_gain, w_query, w_keyval, w_out, score_head, lengths, policy_slots):
    tp_index = lax.axis_index("tp")
    local_rows = residual_in.shape[1]
    resid = residual_in[0].astype(jnp.float32)
    meansq = jnp.mean(resid * resid, axis=-1, keepdims=True)
    normed = (resid * lax.rsqrt(meansq + 1e-05) * norm_gain.astype(jnp.float32)).astype(
        jnp.bfloat16
    )
    query_cols = w_query.shape[1]
    piece = lax.all_gather(normed, "tp", axis=0, tiled=True)
    query_part = jnp.dot(piece, w_query, preferred_element_type=jnp.float32).astype(jnp.bfloat16)
    pair_part = jnp.dot(piece, w_keyval, preferred_element_type=jnp.float32).astype(jnp.bfloat16)
    projected = jnp.concatenate([query_part, pair_part], axis=1)
    queries = projected[:, :query_cols]
    keyval_local = projected[:, query_cols:]
    keyval_full = collect(keyval_local, "tp", 1)
    seq_total = keyval_full.shape[0]
    heads_here = query_cols // HS
    group = QH // KVH
    rowpos = jnp.arange(seq_total, dtype=jnp.int32)[:, None]
    colpos = jnp.arange(seq_total, dtype=jnp.int32)[None, :]
    length = lengths[0]
    valid = (colpos <= rowpos) & (colpos < length)
    outputs = []
    for local_head in range(heads_here):
        head_id = tp_index * heads_here + local_head
        kv_head = head_id // group
        keys = lax.dynamic_slice_in_dim(keyval_full, kv_head * HS, HS, 1)
        values = lax.dynamic_slice_in_dim(keyval_full, KW + kv_head * HS, HS, 1)
        query_head = queries[:, local_head * HS : (local_head + 1) * HS]
        scores = lax.dot_general(
            query_head, keys, (((1,), (1,)), ((), ())), preferred_element_type=jnp.float32
        ) * HS ** (-0.5)
        scores = jnp.where(valid, scores, -1e30)
        probs = jax.nn.softmax(scores, axis=-1).astype(jnp.bfloat16)
        outputs.append(
            jnp.dot(probs, values, preferred_element_type=jnp.float32).astype(jnp.bfloat16)
        )
    attended = jnp.concatenate(outputs, axis=1)
    summed = lax.psum_scatter(
        jnp.dot(attended, w_out, preferred_element_type=jnp.float32).astype(jnp.bfloat16),
        "tp",
        scatter_dimension=0,
        tiled=True,
    ).astype(jnp.float32)
    hidden = (resid + summed).astype(jnp.bfloat16)
    local_last = length - 1 - tp_index * local_rows
    picker = (jnp.arange(local_rows, dtype=jnp.int32) == local_last).astype(jnp.float32)
    weights = picker + seq_total ** (-0.5)
    row_scores = jnp.sum(
        hidden.astype(jnp.float32) * score_head.astype(jnp.float32)[None, :], axis=1
    )
    contrib = jnp.sum(row_scores * weights)
    reward = taken_together(contrib, "tp")
    policy_copy = spread(policy_slots, "rep", 0)
    return (hidden[None], reward.reshape(1), policy_copy)


def solution(mesh):
    placed = (
        P("rep", "tp", None),
        P(),
        P(None, "tp"),
        P(None, "tp"),
        P("tp", None),
        P(),
        P("rep"),
        P("rep", None, "tp"),
    )
    return jax.shard_map(
        on_device,
        mesh=mesh,
        in_specs=placed,
        out_specs=(P("rep", "tp", None), P("rep"), P("rep", None, "tp")),
        check_vma=False,
    )
```

profile of v0, /device:TPU:32, one launch (start us, length us, event | category | flops | bytes accessed | tf_op | source)
XLA Modules:
  0.0 312.6 jit_solution(8463891104759739555)
XLA Ops:
  8.0 0.0 copy-start
  8.0 0.0 reduce-scatter.5.cloned.1.call-start
  8.1 0.0 copy-start.2
  8.1 0.0 copy-start.1
  8.1 1.3 select_bitcast_fusion
  9.3 0.0 reduce-scatter.5.cloned.1.call-update
  9.4 0.0 all-gather.3.cloned.1.call-start
  9.4 0.0 copy-done.2
  9.4 0.6 copy-done.1
  10.0 0.3 fusion
  10.3 1.3 fusion.2
  11.6 0.0 all-gather.3.cloned.1.call-update
  11.6 0.0 all-gather.5.cloned.1.call-start
  12.4 65.2 %reduce-scatter.5.cloned.1.call-done = bf16[48,1024]{1,0:T(8,128)(2,1)} async-done(((bf16[768,1024]{1,0:T(8,128)(2,1)}), bf16[48,1024]{1,0:T(8,128)(2,1)}) %reduce-scatter.5.cloned.1.call-update) | async-done | bytes 98320 | tf_op jit(solution)/shard_map/reduce_scatter | solution.py:44
  77.7 0.0 all-gather.5.cloned.1.call-update
  77.7 48.9 %all-gather.3.cloned.1.call-done = bf16[512,8192]{1,0:T(8,128)(2,1)} async-done(((bf16[64,8192]{1,0:T(8,128)(2,1)}), bf16[512,8192]{1,0:T(8,128)(2,1)}) %all-gather.3.cloned.1.call-update) | async-done | bytes 8388624 | tf_op jit(solution)/shard_map/all_gather | solution.py:57
  126.6 0.0 copy-done
  126.6 5.7 %convolution_convert_fusion.6 = bf16[512,128]{1,0:T(8,128)(2,1)S(1)} fusion(bf16[512,8192]{1,0:T(8,128)(2,1)} %all-gather.3.cloned.1.call-done, bf16[8192,128]{1,0:T(8,128)(2,1)S(1)} %copy-done), kind=kOutput, calls=%fused_computation.23 | convolution fusion | flops 1073807360 | bytes 10616832 | tf_op jit(solution)/shard_map/dot_general | solution.py:59
  132.3 0.1 copy.13
  132.4 1.1 broadcast_in_dim.15
  133.5 4.3 %all-to-all-start = ((bf16[8,512,128]{1,2,0:T(8,128)(2,1)}), bf16[8,512,128]{1,2,0:T(8,128)(2,1)}, u32[]{:S(2)}, u32[]{:S(2)}) async-start(bf16[8,512,128]{1,2,0:T(8,128)(2,1)} %broadcast_in_dim.15), calls=%async_computation | async-start | bytes 2097152 | tf_op jit(solution)/shard_map/all_to_all | solution.py:14
  137.7 0.0 reduce-scatter.3.cloned.1.call-start
  137.8 11.2 %convolution_convert_fusion.1 = bf16[512,512]{1,0:T(8,128)(2,1)} fusion(bf16[512,8192]{1,0:T(8,128)(2,1)} %all-gather.3.cloned.1.call-done, bf16[8192,512]{1,0:T(8,128)(2,1)} %param.10), kind=kOutput, calls=%fused_computation.18 | convolution fusion | flops 4295229440 | bytes 17301504 | tf_op jit(solution)/shard_map/dot_general | solution.py:58
  148.9 6.6 %all-to-all-done = bf16[8,512,128]{1,2,0:T(8,128)(2,1)} async-done(((bf16[8,512,128]{1,2,0:T(8,128)(2,1)}), bf16[8,512,128]{1,2,0:T(8,128)(2,1)}, u32[]{:S(2)}, u32[]{:S(2)}) %all-to-all-start) | async-done | bytes 1048608 | tf_op jit(solution)/shard_map/all_to_all | solution.py:14
  155.5 0.0 copy-start.4
  155.5 1.4 fusion.48
  156.9 1.3 fusion.47
  158.3 0.0 copy-done.4
  158.3 1.3 fusion.46
  159.6 0.2 fusion.9
  159.8 0.2 fusion.10
  160.0 0.2 fusion.11
  160.1 1.3 fusion.45
  161.4 0.2 fusion.12
  161.6 0.0 slice-start
  161.6 1.4 convolution_convert_fusion.5
  163.0 1.2 convolution_convert_fusion.4
  164.3 0.0 slice-start.1
  164.3 1.4 convolution_convert_fusion.3
  165.7 1.2 convolution_convert_fusion.2
  167.0 0.0 slice-done
  167.0 0.0 slice-done.1
  167.0 7.0 %convolution_convert_fusion = bf16[512,8192]{1,0:T(8,128)(2,1)} fusion(bf16[512,8192]{1,0:T(8,128)(2,1)S(1)} %bitcast.27, bf16[512,128]{0,1:T(8,128)(2,1)S(1)} %convolution_convert_fusion.2, bf16[512,128]{0,1:T(8,128)(2,1)S(1)} %convolution_convert_fusion.3, bf16[512,128]{0,1:T(8,128)(2,1)S(1)} %convolution_convert_fusion.4, ...), kind=kOutput, calls=%fused_computation | convolution fusion | flops 4301258752 | bytes 17301504 | tf_op jit(solution)/shard_map/dot_general | solution.py:88
  174.0 0.0 copy-start.3
  174.0 0.0 reduce-scatter.3.cloned.1.call-update
  174.0 0.7 copy-done.3
  174.7 0.0 all-gather.5.cloned.1.call-done
  174.7 112.1 %reduce-scatter.3.cloned.1.call-done = bf16[64,8192]{1,0:T(8,128)(2,1)} async-done(((bf16[512,8192]{1,0:T(8,128)(2,1)}), bf16[64,8192]{1,0:T(8,128)(2,1)}) %reduce-scatter.3.cloned.1.call-update) | async-done | bytes 1048592 | tf_op jit(solution)/shard_map/reduce_scatter | solution.py:87
  286.8 2.7 multiply_reduce_fusion
  289.4 0.6 fusion.43
  290.1 0.6 broadcast_in_dim.18
  290.7 11.0 %all_to_all.11 = f32[8,1,1]{2,1,0:T(1,128)S(1)} all-to-all(f32[8,1,1]{2,1,0:T(1,128)S(1)} %broadcast_in_dim.18), channel_id=1, replica_groups=mesh['rep'=16,'tp'=8] {'tp'}, dimensions={0} | all-to-all | bytes 64 | tf_op jit(solution)/shard_map/all_to_all | solution.py:14
  301.7 0.6 reduce_sum.79
  302.3 2.7 copy.18
  (5 shorter events, 0.0 us)
Async XLA Ops:
  8.0 118.6 %copy-start = (bf16[8192,128]{1,0:T(8,128)(2,1)S(1)}, bf16[8192,128]{1,0:T(8,128)(2,1)}, u32[]{:S(2)}) copy-start(bf16[8192,128]{1,0:T(8,128)(2,1)} %param.11) | copy-start | bytes 6291460
  8.0 69.6 %reduce-scatter.5.cloned.1.call-start = ((), (), s32[]{:S(2)}) async-start(), calls=%async_computation.6 | async-start | bytes 1671168 | tf_op jit(solution)/shard_map/reduce_scatter | solution.py:44
  8.1 1.4 copy-start.2
  8.1 1.9 copy-start.1
  9.4 117.2 %all-gather.3.cloned.1.call-start = ((), (), s32[]{:S(2)}) async-start(), calls=%async_computation.4 | async-start | bytes 9437184 | tf_op jit(solution)/shard_map/all_gather | solution.py:57
  11.6 163.1 %all-gather.5.cloned.1.call-start = ((), (), s32[]{:S(2)}) async-start(), calls=%async_computation.7 | async-start | bytes 1671168 | tf_op jit(solution)/shard_map/all_gather | solution.py:45
  133.5 22.1 %all-to-all-start = ((bf16[8,512,128]{1,2,0:T(8,128)(2,1)}), bf16[8,512,128]{1,2,0:T(8,128)(2,1)}, u32[]{:S(2)}, u32[]{:S(2)}) async-start(bf16[8,512,128]{1,2,0:T(8,128)(2,1)} %broadcast_in_dim.15), calls=%async_computation | async-start | bytes 2097152 | tf_op jit(solution)/shard_map/all_to_all | solution.py:14
  137.7 149.1 %reduce-scatter.3.cloned.1.call-start = ((), (), s32[]{:S(2)}) async-start(), calls=%async_computation.5 | async-start | bytes 9437184 | tf_op jit(solution)/shard_map/reduce_scatter | solution.py:87
  155.5 2.7 copy-start.4
  161.6 5.3 %slice-start = ((s8[8388608]{0:T(1024)(128)(4,1)}), s8[4194304]{0:T(1024)(128)(4,1)S(1)}, s32[]{:S(2)}) async-start(s8[8388608]{0:T(1024)(128)(4,1)} %bitcast.26), calls=%async_computation.8 | async-start | bytes 8388608
  164.3 2.7 slice-start.1
  174.0 0.7 copy-start.3
Sparse Core Ops, SparseCore 0:
  11.8 65.8 reduce-scatter.4
Sparse Core Ops, SparseCore 1:
  12.8 113.7 all-gather.2
  128.1 37.7 all-gather.4
  174.1 112.6 reduce-scatter.2
where the time goes:
time: 314 us; the launch traced here: 313 us
  waiting for transfers between devices  233 us (74%)
  matrix products  34.4 us (11%)
  between operations  16.5 us (5%)
  blocking collectives  11 us (4%)
  other arithmetic  7.55 us (2%)
  local copies, waits for them, and re-layouts  5.78 us (2%)
  starting transfers between devices  4.42 us (1%)
    reduce_scatter x1, waiting for transfers between devices, on_device(): lax.psum_scatter(jnp.dot(attended, w_out, preferred_element_type=jnp.floa...  112 us
    reduce_scatter x1, waiting for transfers between devices, spread(): own = lax.psum_scatter(padded, axis, scatter_dimension=0, tiled=True)  65.2 us
    all_gather x1, waiting for transfers between devices, on_device(): piece = lax.all_gather(normed, 'tp', axis=0, tiled=True)  48.9 us
    dot_general x1, matrix products, on_device(): jnp.dot(piece, w_query, preferred_element_type=jnp.float32)  11.2 us
    all_to_all x1, blocking collectives, sent_to_all(): lax.all_to_all(jnp.broadcast_to(value[None], (length, *value.shape)), axi...  11 us
    dot_general x1, matrix products, on_device(): jnp.dot(attended, w_out, preferred_element_type=jnp.float32)  7 us
    all_to_all x1, waiting for transfers between devices, sent_to_all(): lax.all_to_all(jnp.broadcast_to(value[None], (length, *value.shape)), axi...  6.62 us
  transfers between devices with their start and end apart: 5, of which 4 were waited for; matrix products, arithmetic and copies ran while one was open for 12% of the time, Pallas kernels for 0%

commit v1 on v0

v1 whole, which is shorter than its diff:
```python
import functools

import jax
import jax.numpy as jnp
from jax import lax
from jax.experimental import pallas as pl
from jax.experimental.pallas import tpu as pltpu
from jax.sharding import PartitionSpec as P

HS = 128
N = 8
D = 8192
CW = D // N
ROWS = 64
PLANE = 256
QC = 512
WC = QC + 128
PCH = 8
LAG = 1
MESH = pl.DeviceIdType.MESH
BF = jnp.bfloat16
F32 = jnp.float32


def rcopy(src, dst, ssem, rsem, dev):
    return pltpu.make_async_remote_copy(
        src_ref=src, dst_ref=dst, send_sem=ssem, recv_sem=rsem, device_id=dev, device_id_type=MESH
    )


def when_in(value, low, high, fn):
    @pl.when((value >= low) & (value < high))
    def _():
        fn(value)


class Place:
    def __init__(self):
        rep = lax.axis_index("rep")
        tp = lax.axis_index("tp")
        self.rep, self.tp = rep, tp
        self.core = core = lax.rem(rep, 2)
        self.y = y = lax.rem(rep // 2, 4)
        self.zl = zl = rep // 8
        self.x = x = lax.rem(tp, 4)
        self.zh = zh = tp // 4
        self.xp, self.xm, self.xo = lax.rem(x + 1, 4), lax.rem(x + 3, 4), lax.rem(x + 2, 4)
        self.yp, self.ym, self.yo = lax.rem(y + 1, 4), lax.rem(y + 3, 4), lax.rem(y + 2, 4)
        self.xr = (rep, zh * 4 + self.xp)
        self.xl = (rep, zh * 4 + self.xm)
        self.yr = ((zl * 4 + self.yp) * 2 + core, tp)
        self.yl = ((zl * 4 + self.ym) * 2 + core, tp)
        self.cross = (((1 - zl) * 4 + y) * 2 + core, (1 - zh) * 4 + x)
        self.zpart = (((1 - zl) * 4 + y) * 2 + core, tp)
        self.sib = (rep + 1 - 2 * core, tp)


class Exchange:
    def __init__(self, p, near, far, rows, sems):
        self.p, self.near, self.far, self.rows = p, near, far, rows
        (self.cs, self.cr, self.y1s, self.y1r, self.y2s, self.y2r, self.zs, self.zr, self.ds, self.dr) = sems

    def piece(self, yy, core, part=0, parts=1):
        size = self.rows // 8 // parts
        start = yy * (self.rows // 4) + core * (self.rows // 8) + part * size
        return pl.ds(pl.multiple_of(start, 16), size)

    def move(self, k, where, ssem, rsem, dev):
        ref = self.far.at[k, where]
        return rcopy(ref, ref, ssem, rsem, dev)

    def over_z(self, k):
        p = self.p
        where = self.piece(p.y, p.core)
        return rcopy(self.near.at[k, where], self.far.at[k, where], self.cs.at[k], self.cr.at[k], p.cross)

    def along_y(self, d, k):
        p = self.p
        return self.move(k, self.piece(p.y, p.core), self.y1s.at[d, k], self.y1r.at[d, k], p.yl if d else p.yr)

    def along_y_in(self, d, k):
        p = self.p
        return self.move(k, self.piece(p.yp if d else p.ym, p.core), self.y1s.at[d, k], self.y1r.at[d, k], p.sib)

    def onward_y(self, d, k):
        p = self.p
        where = self.piece(p.yp if d else p.ym, p.core, 2 * p.zl + d, 4)
        return self.move(k, where, self.y2s.at[d, k], self.y2r.at[d, k], p.yl if d else p.yr)

    def onward_y_in(self, d, k):
        p = self.p
        where = self.piece(p.yo, p.core, 2 * p.zl + d, 4)
        return self.move(k, where, self.y2s.at[d, k], self.y2r.at[d, k], p.sib)

    def to_zpart(self, k):
        p = self.p
        return self.move(k, self.piece(p.yo, p.core, p.zl, 2), self.zs.at[k], self.zr.at[k], p.zpart)

    def to_zpart_in(self, k):
        p = self.p
        return self.move(k, self.piece(p.yo, p.core, 1 - p.zl, 2), self.zs.at[k], self.zr.at[k], p.zpart)

    def to_sib(self, j, k, core):
        p = self.p
        where = (
            self.piece(p.y, core),
            self.piece(p.ym, core),
            self.piece(p.yp, core),
            self.piece(p.yo, core, p.zl, 2),
            self.piece(p.yo, core, 1 - p.zl, 2),
        )[j]
        return self.move(k, where, self.ds.at[j, k], self.dr.at[j, k], p.sib)

    def stage0(self, k):
        self.over_z(k).wait_recv()
        for d in (0, 1):
            self.along_y(d, k).start()
        self.to_sib(0, k, self.p.core).start()

    def stage1(self, k):
        for d in (0, 1):
            self.along_y_in(d, k).wait_recv()
            self.onward_y(d, k).start()
            self.to_sib(1 + d, k, self.p.core).start()

    def stage2(self, k):
        for d in (0, 1):
            self.onward_y_in(d, k).wait_recv()
        self.to_zpart(k).start()
        self.to_sib(3, k, self.p.core).start()

    def stage3(self, k):
        self.to_zpart_in(k).wait_recv()
        self.to_sib(4, k, self.p.core).start()

    def ready(self, k):
        for j in range(5):
            self.to_sib(j, k, 1 - self.p.core).wait_recv()

    def drain(self, k):
        self.over_z(k).wait_send()
        for d in (0, 1):
            self.along_y(d, k).wait_send()
            self.onward_y(d, k).wait_send()
        self.to_zpart(k).wait_send()
        for j in range(5):
            self.to_sib(j, k, self.p.core).wait_send()

    def stages(self, i):
        for s, stage in enumerate((self.stage0, self.stage1, self.stage2, self.stage3)):
            when_in(i - s, 0, N, stage)


def kernel(
    gain, head, length, resid_h, wq_h, wkv_h, wo_h, pol_h,
    hid_o, rew_o, pol_o,
    rv, tok, wl, wr, ol, fr, acc, qv, kvs, kva, att, part, r1, r2, hid, racc, rsend, rrecv, pol,
    lsem, wsem, osem, t1s, t1r, t2s, t2r,
    acs, acr, ay1s, ay1r, ay2s, ay2r, azs, azr, ads, adr,
    bcs, bcr, by1s, by1r, by2s, by2r, bzs, bzr, bds, bdr,
    ks, kr, s1s, s1r, s2s, s2r, hsem, ws, wrs, ps, pr, psem,
):
    p = Place()
    ea = Exchange(p, wl, wr, CW, (acs, acr, ay1s, ay1r, ay2s, ay2r, azs, azr, ads, adr))
    eb = Exchange(p, ol, fr, 512, (bcs, bcr, by1s, by1r, by2s, by2r, bzs, bzr, bds, bdr))

    barrier = pltpu.get_barrier_semaphore()
    for t in range(8):
        @pl.when(t != p.tp)
        def _():
            pl.semaphore_signal(barrier, inc=1, device_id=(p.rep, t), device_id_type=MESH)
    for dev in (p.yr, p.yl, p.cross, p.zpart, p.sib):
        pl.semaphore_signal(barrier, inc=1, device_id=dev, device_id_type=MESH)

    def load_resid(k):
        return pltpu.make_async_copy(resid_h.at[:, pl.ds(k * CW, CW)], rv.at[k], lsem.at[k])

    def load_wq(k):
        at = pl.ds(pl.multiple_of(k * CW, CW), CW)
        return pltpu.make_async_copy(wq_h.at[at], wl.at[k, :, pl.ds(0, QC)], wsem.at[0, k])

    def load_wkv(k):
        at = pl.ds(pl.multiple_of(k * CW, CW), CW)
        return pltpu.make_async_copy(wkv_h.at[at], wl.at[k, :, pl.ds(QC, 128)], wsem.at[1, k])

    def load_wo(k):
        at = pl.ds(pl.multiple_of(k * CW, CW), CW)
        return pltpu.make_async_copy(wo_h.at[:, at], ol.at[k], osem.at[k])

    root = (p.zl == 0) & (p.y == 0) & (p.core == 0)
    load_pol = pltpu.make_async_copy(pol_h, pol, psem)

    for k in range(N):
        load_resid(k).start()

    @pl.loop(0, N)
    def _(k):
        load_wq(k).start()
        load_wkv(k).start()

    @pl.loop(0, N)
    def _(k):
        load_wo(k).start()

    @pl.when(root)
    def _():
        load_pol.start()

    own = pl.ds(pl.multiple_of(p.x * ROWS, ROWS), ROWS)
    squares = jnp.zeros((ROWS, 1), F32)
    for k in range(N):
        load_resid(k).wait()
        r = rv[k].astype(F32)
        squares += jnp.sum(r * r, axis=-1, keepdims=True)
    scale = lax.rsqrt(squares / D + 1e-05)
    for k in range(N):
        tok[k, own, :] = (rv[k].astype(F32) * scale * gain[:, k * CW : (k + 1) * CW].astype(F32)).astype(BF)

    pl.semaphore_wait(barrier, 12)

    def block(xx, start=0, size=ROWS):
        return pl.ds(pl.multiple_of(xx * ROWS + start, 16), size)

    def token_copy(k, where, ssem, rsem, d):
        ref = tok.at[k, where]
        return rcopy(ref, ref, ssem.at[d, k], rsem.at[d, k], p.xl if d else p.xr)

    def token_out(d, k):
        return token_copy(k, block(p.x), t1s, t1r, d)

    def token_in(d, k):
        return token_copy(k, block(p.xp if d else p.xm), t1s, t1r, d)

    def token_onward(d, k):
        return token_copy(k, block(p.xp if d else p.xm, 32 * d, 32), t2s, t2r, d)

    def token_onward_in(d, k):
        return token_copy(k, block(p.xo, 32 * d, 32), t2s, t2r, d)

    def tokens_send(k):
        for d in (0, 1):
            token_out(d, k).start()

    def tokens_forward(k):
        for d in (0, 1):
            token_in(d, k).wait_recv()
            token_onward(d, k).start()

    @pl.loop(0, N)
    def _(k):
        load_wq(k).wait()
        load_wkv(k).wait()
        ea.over_z(k).start()

    for k in range(2):
        tokens_send(k)

    acc[...] = jnp.zeros_like(acc)

    def project(k):
        for d in (0, 1):
            token_onward_in(d, k).wait_recv()
        ea.ready(k)
        acc[p.zh] = acc[p.zh] + jnp.dot(tok[k], wl[k], preferred_element_type=F32)
        acc[1 - p.zh] = acc[1 - p.zh] + jnp.dot(tok[k], wr[k], preferred_element_type=F32)

    def open_b(k):
        load_wo(k).wait()
        eb.over_z(k).start()

    @pl.loop(0, N + 4)
    def _(i):
        when_in(i, 0, N, open_b)
        when_in(i + 2, 0, N, tokens_send)
        when_in(i - 1, 0, N, tokens_forward)
        ea.stages(i)
        eb.stages(i - N)
        when_in(i - 4, 0, N, project)

    kvs[:, 0:HS] = acc[0, :, QC:].astype(BF)
    kvs[:, HS:] = acc[1, :, QC:].astype(BF)
    slot = p.x // 2
    here = pl.ds(pl.multiple_of(p.zh * PLANE, PLANE), PLANE)

    def kv_copy(i):
        xd, zd = 2 * lax.rem(p.x, 2) + i // 2, i % 2
        to = zd * 4 + xd
        return to, rcopy(kvs, kva.at[slot, here], ks.at[i], kr.at[slot * 2 + p.zh], (p.rep, to))

    for i in range(4):
        to, copy = kv_copy(i)

        @pl.when(to != p.tp)
        def _():
            copy.start()

        @pl.when(to == p.tp)
        def _():
            kva[slot, here, :] = kvs[...]

    for s in (0, 1):
        qv[s] = acc[s, :, :QC].astype(BF)
    eb.stages(jnp.int32(4))
    for j in (0, 1):
        for pz in (0, 1):
            @pl.when(pz * 4 + 2 * j + p.x // 2 != p.tp)
            def _():
                ref = kva.at[j, pl.ds(pz * PLANE, PLANE)]
                rcopy(ref, ref, ks.at[0], kr.at[j * 2 + pz], p.sib).wait_recv()

    rowpos = lax.broadcasted_iota(jnp.int32, (PLANE, 512), 0) + p.zh * PLANE
    colpos = lax.broadcasted_iota(jnp.int32, (PLANE, 512), 1)
    last = length[0]
    valid = (colpos <= rowpos) & (colpos < last)
    for s in (0, 1):
        for h in range(4):
            cols = slice(h * HS, (h + 1) * HS)
            scores = lax.dot_general(
                qv[s, :, cols], kva[s, :, 0:HS], (((1,), (1,)), ((), ())), preferred_element_type=F32
            ) * HS ** (-0.5)
            scores = jnp.where(valid, scores, -1e30)
            top = jnp.max(scores, axis=-1, keepdims=True)
            weight = jnp.exp(scores - top)
            probs = (weight / jnp.sum(weight, axis=-1, keepdims=True)).astype(BF)
            att[s, :, cols] = jnp.dot(probs, kva[s, :, HS:], preferred_element_type=F32).astype(BF)
        eb.stages(jnp.int32(5 + s))

    HALF = CW // 2

    def half_copy(d, c):
        src = part.at[c, block(p.xo), pl.ds(d * HALF, HALF)]
        return rcopy(src, r1.at[d, c], s1s.at[d, c], s1r.at[d, c], p.xl if d else p.xr)

    def full_copy(d, c):
        src = part.at[c, block(p.xm if d else p.xp)]
        return rcopy(src, r2.at[d, c], s2s.at[d, c], s2r.at[d, c], p.xl if d else p.xr)

    def hid_copy(c):
        at = pl.ds(pl.multiple_of(c * CW, CW), CW)
        return pltpu.make_async_copy(hid.at[c], hid_o.at[:, at], hsem.at[c])

    def out_project(c):
        eb.ready(c)
        part[c] = (
            jnp.dot(att[p.zh], ol[c], preferred_element_type=F32)
            + jnp.dot(att[1 - p.zh], fr[c], preferred_element_type=F32)
        ).astype(BF)
        for d in (0, 1):
            half_copy(d, c).start()

    def pass_on(c):
        for d in (0, 1):
            half_copy(d, c).wait_recv()
            rows, cols = block(p.xm if d else p.xp), pl.ds(d * HALF, HALF)
            part[c, rows, cols] = (part[c, rows, cols].astype(F32) + r1[d, c].astype(F32)).astype(BF)
            full_copy(d, c).start()

    def finish(c):
        for d in (0, 1):
            full_copy(d, c).wait_recv()
        summed = part[c, own, :].astype(F32) + r2[0, c].astype(F32) + r2[1, c].astype(F32)
        out = (rv[c].astype(F32) + summed).astype(BF)
        hid[c] = out
        racc[...] = racc[...] + out.astype(F32) * head[:, pl.ds(pl.multiple_of(c * CW, CW), CW)].astype(F32)
        hid_copy(c).start()

    first = (p.zl == 0) & (p.core == 0)

    def pol_copy(way, m, dev):
        return rcopy(pol.at[m], pol.at[m], ps.at[way, m], pr.at[m], dev)

    def pol_fan(m):
        pol_copy(1, m, p.zpart).start()
        pol_copy(2, m, p.sib).start()

    ups = p.y < 3
    downs = (p.y == 0) | (p.y > 1)
    hops = (p.y, lax.rem(4 - p.y, 4))

    def pol_step(it):
        @pl.when(root & (it == 0))
        def _():
            load_pol.wait()
            for m in range(4):
                pol_copy(0, m, p.yr).start()
                pol_copy(0, 4 + m, p.yl).start()
            for m in range(PCH):
                pol_fan(m)

        for d in (0, 1):
            m = it - LAG * hops[d]

            @pl.when(first & (p.y > 0) & (m >= 0) & (m < 4))
            def _():
                pol_copy(0, 4 * d + m, p.yr).wait_recv()

                @pl.when(downs if d else ups)
                def _():
                    pol_copy(0, 4 * d + m, p.yl if d else p.yr).start()

                pol_fan(4 * d + m)

            m2 = m - LAG

            @pl.when((p.zl == 1) & (p.core == 0) & (m2 >= 0) & (m2 < 4))
            def _():
                pol_copy(1, 4 * d + m2, p.zpart).wait_recv()
                pol_copy(2, 4 * d + m2, p.sib).start()

    racc[...] = jnp.zeros_like(racc)

    @pl.loop(0, max(N + 2, 4 * LAG + 4))
    def _(it):
        eb.stages(it + 7)
        when_in(it, 0, N, out_project)
        when_in(it - 1, 0, N, pass_on)
        when_in(it - 2, 0, N, finish)
        pol_step(it)

    @pl.when(p.core == 1)
    def _():
        for m in range(PCH):
            pol_copy(2, m, p.sib).wait_recv()

    store_pol = pltpu.make_async_copy(pol, pol_o, psem)
    store_pol.start()

    rows = jnp.sum(racc[...], axis=-1, keepdims=True)
    position = lax.broadcasted_iota(jnp.int32, (ROWS, 1), 0) + p.tp * ROWS
    picked = jnp.where(position == last - 1, 1.0, 0.0) + 512 ** (-0.5)
    share = jnp.sum(rows * picked, axis=0, keepdims=True)
    rsend[...] = jnp.broadcast_to(share, (8, 128))

    def reward_copy(t):
        return rcopy(rsend, rrecv.at[p.tp], ws.at[t], wrs.at[p.tp], (p.rep, t))

    for t in range(8):
        @pl.when(t != p.tp)
        def _():
            reward_copy(t).start()

    @pl.loop(0, N)
    def _(k):
        ea.drain(k)
        eb.drain(k)
        for d in (0, 1):
            token_out(d, k).wait_send()
            token_onward(d, k).wait_send()
            half_copy(d, k).wait_send()
            full_copy(d, k).wait_send()
        hid_copy(k).wait()

    for i in range(4):
        to, copy = kv_copy(i)

        @pl.when(to != p.tp)
        def _():
            copy.wait_send()

    for m in range(PCH):
        @pl.when(first & (downs if m >= 4 else ups))
        def _():
            pol_copy(0, m, p.yr).wait_send()

        @pl.when(first)
        def _():
            pol_copy(1, m, p.zpart).wait_send()

        @pl.when(p.core == 0)
        def _():
            pol_copy(2, m, p.sib).wait_send()

    total = jnp.zeros((8, 128), F32)
    for t in range(8):
        @pl.when(t != p.tp)
        def _():
            rcopy(rsend, rrecv.at[t], ws.at[t], wrs.at[t], (p.rep, t)).wait_recv()
            reward_copy(t).wait_send()

        @pl.when(t == p.tp)
        def _():
            rrecv[t] = rsend[...]

        total += rrecv[t]
    rew_o[...] = total
    store_pol.wait()


def on_device(residual_in, norm_gain, w_query, w_keyval, w_out, score_head, lengths, policy_slots):
    vmem = pl.BlockSpec(memory_space=pltpu.VMEM)
    smem = pl.BlockSpec(memory_space=pltpu.SMEM)
    hbm = pl.BlockSpec(memory_space=pl.ANY)
    dma = pltpu.SemaphoreType.DMA

    def exchange_sems():
        return [dma((N,)), dma((N,)), dma((2, N)), dma((2, N)), dma((2, N)), dma((2, N)),
                dma((N,)), dma((N,)), dma((5, N)), dma((5, N))]

    prow = policy_slots.shape[1]
    hidden, reward, policy = pl.pallas_call(
        kernel,
        out_shape=(
            jax.ShapeDtypeStruct((ROWS, D), BF),
            jax.ShapeDtypeStruct((8, 128), F32),
            jax.ShapeDtypeStruct((PCH, prow // PCH, 1024), BF),
        ),
        in_specs=[vmem, vmem, smem, hbm, hbm, hbm, hbm, hbm],
        out_specs=(hbm, vmem, hbm),
        scratch_shapes=[
            pltpu.VMEM((N, ROWS, CW), BF),
            pltpu.VMEM((N, PLANE, CW), BF),
            pltpu.VMEM((N, CW, WC), BF),
            pltpu.VMEM((N, CW, WC), BF),
            pltpu.VMEM((N, 512, CW), BF),
            pltpu.VMEM((N, 512, CW), BF),
            pltpu.VMEM((2, PLANE, WC), F32),
            pltpu.VMEM((2, PLANE, QC), BF),
            pltpu.VMEM((PLANE, 2 * HS), BF),
            pltpu.VMEM((2, 2 * PLANE, 2 * HS), BF),
            pltpu.VMEM((2, PLANE, QC), BF),
            pltpu.VMEM((N, PLANE, CW), BF),
            pltpu.VMEM((2, N, ROWS, CW // 2), BF),
            pltpu.VMEM((2, N, ROWS, CW), BF),
            pltpu.VMEM((N, ROWS, CW), BF),
            pltpu.VMEM((ROWS, CW), F32),
            pltpu.VMEM((8, 128), F32),
            pltpu.VMEM((8, 8, 128), F32),
            pltpu.VMEM((PCH, prow // PCH, 1024), BF),
            dma((N,)), dma((2, N)), dma((N,)),
            dma((2, N)), dma((2, N)), dma((2, N)), dma((2, N)),
            *exchange_sems(),
            *exchange_sems(),
            dma((4,)), dma((4,)),
            dma((2, N)), dma((2, N)), dma((2, N)), dma((2, N)),
            dma((N,)), dma((8,)), dma((8,)), dma((3, PCH)), dma((PCH,)), dma,
        ],
        compiler_params=pltpu.CompilerParams(
            collective_id=0, has_side_effects=True, vmem_limit_bytes=66_000_000
        ),
        name="block",
    )(
        norm_gain.reshape(1, D), score_head.reshape(1, D), lengths,
        residual_in[0], w_query, w_keyval, w_out, policy_slots[0].reshape(PCH, prow // PCH, 1024),
    )
    return hidden[None], reward[0, :1], policy.reshape(1, prow, 1024)


def solution(mesh):
    placed = (
        P("rep", "tp", None),
        P(),
        P(None, "tp"),
        P(None, "tp"),
        P("tp", None),
        P(),
        P("rep"),
        P("rep", None, "tp"),
    )
    return jax.shard_map(
        on_device,
        mesh=mesh,
        in_specs=placed,
        out_specs=(P("rep", "tp", None), P("rep"), P("rep", None, "tp")),
        check_vma=False,
    )
```

time: 314 us -> 152 us (0.48)
  waiting for transfers between devices: 233 us -> 0 us
  Pallas kernels: 0 us -> 143 us
  matrix products: 34.4 us -> 0 us
  between operations: 16.5 us -> 1.3 us
  blocking collectives: 11 us -> 0 us
  other arithmetic: 7.55 us -> 0 us
  starting transfers between devices: 4.42 us -> 0 us
    reduce_scatter x2 -> x0, waiting for transfers between devices: 177 us -> none  [the longest x1 112 us: on_device(): lax.psum_scatter(jnp.dot(attended, w_out, preferred_element_type=jnp.floa...]
    pallas_call x0 -> x1, Pallas kernels: none -> 143 us  [on_device(): pl.pallas_call(kernel, out_shape=(jax.ShapeDtypeStruct((ROWS, D), BF), ja...]
    all_gather x2 -> x0, waiting for transfers between devices: 48.9 us -> none  [the longest x1 48.9 us: on_device(): piece = lax.all_gather(normed, 'tp', axis=0, tiled=True)]
    dot_general x11 -> x0, matrix products: 34.4 us -> none  [the longest x1 11.2 us: on_device(): jnp.dot(piece, w_query, preferred_element_type=jnp.float32)]
    all_to_all x1 -> x0, blocking collectives: 11 us -> none  [sent_to_all(): lax.all_to_all(jnp.broadcast_to(value[None], (length, *value.shape)), axi...]
    all_to_all x1 -> x0, waiting for transfers between devices: 6.62 us -> none  [sent_to_all(): lax.all_to_all(jnp.broadcast_to(value[None], (length, *value.shape)), axi...]
    reduce_sum x8 -> x0, other arithmetic: 4.97 us -> none  [the longest x1 2.66 us: on_device(): jnp.sum(hidden.astype(jnp.float32) * score_head.astype(jnp.float32)[None,...]
    all_to_all x1 -> x0, starting transfers between devices: 4.25 us -> none  [sent_to_all(): lax.all_to_all(jnp.broadcast_to(value[None], (length, *value.shape)), axi...]
  transfers between devices with their start and end apart: 5 -> 0, of which waited for: 4 -> 0; matrix products, arithmetic and copies ran while one was open for 12% -> 0% of each run, Pallas kernels for 0% -> 0%
where the time goes in v1:
time: 152 us
  Pallas kernels  143 us (94%)
  local copies, waits for them, and re-layouts  7.42 us (5%)
    pallas_call x1, Pallas kernels, on_device(): pl.pallas_call(kernel, out_shape=(jax.ShapeDtypeStruct((ROWS, D), BF), ja...  143 us
    unnamed x4, local copies, waits for them, and re-layouts  3.41 us

profile of v1, /device:TPU:32, one launch (start us, length us, event | category | flops | bytes accessed | tf_op | source)
XLA Modules:
  0.0 151.8 jit_solution(8378017504466456617)
XLA Ops:
  1.3 1.4 reshape.15.gain
  2.6 1.3 reshape.16.head
  4.0 143.1 %block.1 = (bf16[64,8192]{1,0:T(8,128)(2,1)}, f32[8,128]{1,0:T(8,128)}, bf16[8,96,1024]{2,1,0:T(8,128)(2,1)}) custom-call(bf16[1,8192]{1,0:T(2,128)(2,1)} %reshape.15.gain, bf16[1,8192]{1,0:T(2,128)(2,1)} %reshape.16.head, s32[1]{0:T(128)S(6)} %copy.13.length, bf16[64,8192]{1,0:T(8,128)(2,1)} %bitcast.7, bf16[8192,512]{1,0:T(8,128)(2,1)} %wq_h.1, ...), custom_call_target="tpu_custom_call" | custom-call | tf_op jit(solution)/shard_map/block/pallas_call | solution.py:500
  147.1 0.0 copy-start
  147.1 1.3 slice.3
  148.4 2.3 %copy.14 = bf16[1,64,8192]{2,1,0:T(8,128)(2,1)} copy(bf16[1,64,8192]{2,1,0:T(8,128)(2,1)} %bitcast.8) | data formatting | bytes 2097152
  150.7 0.0 copy-done
  150.7 1.1 copy.15
Async XLA Ops:
  147.1 3.6 %copy-start = (bf16[8,96,1024]{2,1,0:T(8,128)(2,1)S(1)}, bf16[8,96,1024]{2,1,0:T(8,128)(2,1)}, u32[]{:S(2)}) copy-start(bf16[8,96,1024]{2,1,0:T(8,128)(2,1)} %get-tuple-element.8) | copy-start | bytes 4718596

commit v2 on v1

v2 whole, which is shorter than its diff:
```python
import functools

import jax
import jax.numpy as jnp
from jax import lax
from jax.experimental import pallas as pl
from jax.experimental.pallas import tpu as pltpu
from jax.sharding import PartitionSpec as P

HS = 128
N = 16
D = 8192
CW = D // N
ROWS = 64
PLANE = 256
QC = 512
WC = QC + 128
PCH = 8
LAG = 3
MESH = pl.DeviceIdType.MESH
BF = jnp.bfloat16
F32 = jnp.float32


def rcopy(src, dst, ssem, rsem, dev):
    return pltpu.make_async_remote_copy(
        src_ref=src, dst_ref=dst, send_sem=ssem, recv_sem=rsem, device_id=dev, device_id_type=MESH
    )


def when_in(value, low, high, fn):
    @pl.when((value >= low) & (value < high))
    def _():
        fn(value)


class Place:
    def __init__(self):
        rep = lax.axis_index("rep")
        tp = lax.axis_index("tp")
        self.rep, self.tp = rep, tp
        self.core = core = lax.rem(rep, 2)
        self.y = y = lax.rem(rep // 2, 4)
        self.zl = zl = rep // 8
        self.x = x = lax.rem(tp, 4)
        self.zh = zh = tp // 4
        self.xp, self.xm, self.xo = lax.rem(x + 1, 4), lax.rem(x + 3, 4), lax.rem(x + 2, 4)
        self.yp, self.ym, self.yo = lax.rem(y + 1, 4), lax.rem(y + 3, 4), lax.rem(y + 2, 4)
        self.xr = (rep, zh * 4 + self.xp)
        self.xl = (rep, zh * 4 + self.xm)
        self.yr = ((zl * 4 + self.yp) * 2 + core, tp)
        self.yl = ((zl * 4 + self.ym) * 2 + core, tp)
        self.cross = (((1 - zl) * 4 + y) * 2 + core, (1 - zh) * 4 + x)
        self.zpart = (((1 - zl) * 4 + y) * 2 + core, tp)
        self.sib = (rep + 1 - 2 * core, tp)


class Exchange:
    def __init__(self, p, near, far, rows, sems):
        self.p, self.near, self.far, self.rows = p, near, far, rows
        self.sent, self.cr, self.y1r, self.y2r, self.z1r, self.z2r, self.dr = sems

    def piece(self, yy, core, sub=0, subs=4):
        size = self.rows // 32
        start = yy * (self.rows // 4) + core * (self.rows // 8) + sub * size
        return pl.ds(pl.multiple_of(start, 16), subs * size)

    def move(self, k, where, rsem, dev):
        ref = self.far.at[k, where]
        rcopy(ref, ref, self.sent, rsem.at[k], dev).start()

    def arrived(self, k, count, rsem):
        ref = self.far.at[k, pl.ds(0, count * (self.rows // 32))]
        rcopy(ref, ref, self.sent, rsem.at[k], self.p.sib).wait_recv()

    def over_z(self, k):
        p = self.p
        where = self.piece(p.y, p.core)
        rcopy(self.near.at[k, where], self.far.at[k, where], self.sent, self.cr.at[k], p.cross).start()

    def stage0(self, k):
        p = self.p
        self.arrived(k, 4, self.cr)
        self.move(k, self.piece(p.y, p.core, p.zl, 3), self.y1r, p.yr)
        self.move(k, self.piece(p.y, p.core, p.zl, 3), self.y1r, p.yl)
        self.move(k, self.piece(p.y, p.core), self.dr, p.sib)

    def stage1(self, k):
        p = self.p
        self.arrived(k, 6, self.y1r)
        self.move(k, self.piece(p.ym, p.core, 2 * p.zl, 1), self.y2r, p.yr)
        self.move(k, self.piece(p.yp, p.core, 2 * p.zl + 1, 1), self.y2r, p.yl)
        self.move(k, self.piece(p.ym, p.core, 3 * p.zl, 1), self.z1r, p.zpart)
        self.move(k, self.piece(p.yp, p.core, 3 * p.zl, 1), self.z1r, p.zpart)

    def stage2(self, k):
        p = self.p
        self.arrived(k, 2, self.y2r)
        self.move(k, self.piece(p.yo, p.core, 2 * p.zl, 2), self.z2r, p.zpart)
        self.arrived(k, 2, self.z1r)
        self.move(k, self.piece(p.ym, p.core), self.dr, p.sib)
        self.move(k, self.piece(p.yp, p.core), self.dr, p.sib)

    def stage3(self, k):
        p = self.p
        self.arrived(k, 2, self.z2r)
        self.move(k, self.piece(p.yo, p.core), self.dr, p.sib)

    def ready(self, k):
        self.arrived(k, 16, self.dr)

    def drain(self):
        rcopy(self.far, self.far, self.sent, self.sent, self.p.sib).wait_send()


def kernel(
    gain, head, length, resid_h, wq_h, wkv_h, wo_h, pol_h,
    hid_o, rew_o, pol_o,
    rv, tok, wl, wr, ol, fr, acc, qv, kvs, kva, att, part, r1, r2, hid, racc, rsend, rrecv, pol,
    lsem, wsem, osem, tsent, t1r, t2r,
    asent, acr, ay1r, ay2r, az1r, az2r, adr,
    bsent, bcr, by1r, by2r, bz1r, bz2r, bdr,
    ks, kr, ssent, s1r, s2r, hsem, wsent, wrecv, psent, pr, psem,
):
    p = Place()
    ea = Exchange(p, wl, wr, CW, (asent, acr, ay1r, ay2r, az1r, az2r, adr))
    eb = Exchange(p, ol, fr, QC, (bsent, bcr, by1r, by2r, bz1r, bz2r, bdr))

    barrier = pltpu.get_barrier_semaphore()
    for t in range(8):
        @pl.when(t != p.tp)
        def _():
            pl.semaphore_signal(barrier, inc=1, device_id=(p.rep, t), device_id_type=MESH)
    for dev in (p.yr, p.yl, p.cross, p.zpart, p.sib):
        pl.semaphore_signal(barrier, inc=1, device_id=dev, device_id_type=MESH)

    root = (p.zl == 0) & (p.y == 0) & (p.core == 0)

    for k in range(N):
        pltpu.make_async_copy(resid_h.at[:, pl.ds(k * CW, CW)], rv.at[k], lsem).start()

    @pl.loop(0, N)
    def _(k):
        at = pl.ds(pl.multiple_of(k * CW, CW), CW)
        pltpu.make_async_copy(wq_h.at[at], wl.at[k, :, pl.ds(0, QC)], wsem.at[k]).start()
        pltpu.make_async_copy(wkv_h.at[at], wl.at[k, :, pl.ds(QC, 128)], wsem.at[k]).start()

    @pl.loop(0, N)
    def _(k):
        at = pl.ds(pl.multiple_of(k * CW, CW), CW)
        pltpu.make_async_copy(wo_h.at[:, at], ol.at[k], osem).start()

    load_pol = pltpu.make_async_copy(pol_h, pol, psem)

    @pl.when(root)
    def _():
        load_pol.start()

    own = pl.ds(pl.multiple_of(p.x * ROWS, ROWS), ROWS)
    pltpu.make_async_copy(rv, rv, lsem).wait()
    squares = jnp.zeros((ROWS, 1), F32)
    for k in range(N):
        r = rv[k].astype(F32)
        squares += jnp.sum(r * r, axis=-1, keepdims=True)
    scale = lax.rsqrt(squares / D + 1e-05)
    for k in range(N):
        g = gain[k * CW : (k + 1) * CW].astype(F32).reshape(1, CW)
        tok[k, own, :] = (rv[k].astype(F32) * scale * g).astype(BF)

    pl.semaphore_wait(barrier, 12)

    def block(xx, start=0, size=ROWS):
        return pl.ds(pl.multiple_of(xx * ROWS + start, 16), size)

    def token_move(k, where, rsem, dev):
        ref = tok.at[k, where]
        rcopy(ref, ref, tsent, rsem.at[k], dev).start()

    def token_arrived(k, count, rsem):
        ref = tok.at[k, pl.ds(0, count)]
        rcopy(ref, ref, tsent, rsem.at[k], p.sib).wait_recv()

    def tokens_send(k):
        token_move(k, block(p.x), t1r, p.xr)
        token_move(k, block(p.x), t1r, p.xl)

    def tokens_forward(k):
        token_arrived(k, 2 * ROWS, t1r)
        token_move(k, block(p.xm, 0, 32), t2r, p.xr)
        token_move(k, block(p.xp, 32, 32), t2r, p.xl)

    for k in range(2):
        tokens_send(k)

    @pl.loop(0, N)
    def _(k):
        pltpu.make_async_copy(wl.at[k], wl.at[k], wsem.at[k]).wait()
        ea.over_z(k)

    acc[...] = jnp.zeros_like(acc)

    def project(k):
        token_arrived(k, ROWS, t2r)
        ea.ready(k)
        acc[p.zh] = acc[p.zh] + jnp.dot(tok[k], wl[k], preferred_element_type=F32)
        acc[1 - p.zh] = acc[1 - p.zh] + jnp.dot(tok[k], wr[k], preferred_element_type=F32)

    def step_b(j):
        @pl.when(j == -3)
        def _():
            pltpu.make_async_copy(ol, ol, osem).wait()

        when_in(j + 3, 0, N, eb.over_z)
        when_in(j - 6, 0, N, eb.stage3)
        when_in(j - 5, 0, N, eb.stage2)
        when_in(j - 4, 0, N, eb.stage1)
        when_in(j, 0, N, eb.stage0)

    @pl.loop(0, N + 4)
    def _(i):
        when_in(i + 2, 0, N, tokens_send)
        when_in(i - 1, 0, N, tokens_forward)
        when_in(i - 3, 0, N, ea.stage3)
        when_in(i - 2, 0, N, ea.stage2)
        when_in(i - 1, 0, N, ea.stage1)
        when_in(i, 0, N, ea.stage0)
        step_b(i - N)
        when_in(i - 4, 0, N, project)

    first = (p.zl == 0) & (p.core == 0)
    ups = p.y < 3
    downs = (p.y == 0) | (p.y > 1)
    hops = (p.y, lax.rem(4 - p.y, 4))

    def pol_move(way, m, dev):
        rcopy(pol.at[m], pol.at[m], psent.at[way], pr.at[m], dev).start()

    def pol_arrived(m):
        rcopy(pol.at[m], pol.at[m], psem, pr.at[m], p.sib).wait_recv()

    def pol_fan(m):
        pol_move(2, m, p.zpart)
        pol_move(3, m, p.sib)

    def pol_step(j):
        @pl.when(root & (j == 4))
        def _():
            load_pol.wait()

        for d in (0, 1):
            t = j - 4 - LAG * hops[d]
            m = t // 2

            @pl.when(first & (t >= 0) & (t < 8) & (lax.rem(t, 2) == 0))
            def _():
                @pl.when(p.y > 0)
                def _():
                    pol_arrived(4 * d + m)

                @pl.when(downs if d else ups)
                def _():
                    pol_move(d, 4 * d + m, p.yl if d else p.yr)

                pol_fan(4 * d + m)

            t2 = t - LAG
            m2 = t2 // 2

            @pl.when((p.zl == 1) & (p.core == 0) & (t2 >= 0) & (t2 < 8) & (lax.rem(t2, 2) == 0))
            def _():
                pol_arrived(4 * d + m2)
                pol_move(3, 4 * d + m2, p.sib)

    for kind in (0, 1):
        kvs[kind] = acc[kind, :, QC:].astype(BF)
    slot = p.x // 2
    here = pl.ds(pl.multiple_of(p.zh * PLANE, PLANE), PLANE)
    targets = [(kind, xd, zd) for kind in (0, 1) for zd in (1, 0) for xd in (0, 1)]

    def kv_target(kind, xd, zd):
        to = zd * 4 + 2 * lax.rem(p.x, 2) + xd
        return to, rcopy(
            kvs.at[kind], kva.at[kind, slot, here], ks.at[kind, 2 * zd + xd],
            kr.at[kind, slot * 2 + p.zh], (p.rep, to),
        )

    for target in targets:
        to, copy = kv_target(*target)

        @pl.when((to != p.tp) & (target[2] >= p.zh))
        def _():
            copy.start()

        @pl.when(to == p.tp)
        def _():
            kva[target[0], slot, here, :] = kvs[target[0]]

    for s in (0, 1):
        qv[s] = acc[s, :, :QC].astype(BF)
    step_b(jnp.int32(4))
    pol_step(jnp.int32(4))

    def kv_arrived(kind, planes):
        for j in (0, 1):
            for pz in range(planes):
                @pl.when(pz * 4 + 2 * j + p.x // 2 != p.tp)
                def _():
                    ref = kva.at[kind, j, pl.ds(pz * PLANE, PLANE)]
                    rcopy(ref, ref, ks.at[0, 0], kr.at[kind, j * 2 + pz], p.sib).wait_recv()

    last = length[0]

    def attend(pair, planes):
        keys = planes * PLANE
        rowpos = lax.broadcasted_iota(jnp.int32, (PLANE, keys), 0) + (planes - 1) * PLANE
        colpos = lax.broadcasted_iota(jnp.int32, (PLANE, keys), 1)
        valid = (colpos <= rowpos) & (colpos < last)
        if pair == 0:
            kv_arrived(0, planes)
        for half in (0, 1):
            s, h = pair // 2, 2 * (pair % 2) + half
            cols = slice(h * HS, (h + 1) * HS)
            scores = lax.dot_general(
                qv[s, :, cols], kva[0, s, :keys, :], (((1,), (1,)), ((), ())),
                preferred_element_type=F32,
            )
            scores = jnp.where(valid, scores, -1e30)
            top = jnp.max(scores, axis=-1, keepdims=True)
            weight = jnp.exp2((scores - top) * (HS ** (-0.5) * 1.4426950408889634))
            probs = (weight * (1.0 / jnp.sum(weight, axis=-1, keepdims=True))).astype(BF)
            if pair == 0 and half == 0:
                kv_arrived(1, planes)
            att[s, :, cols] = jnp.dot(probs, kva[1, s, :keys, :], preferred_element_type=F32).astype(BF)

    for pair in range(4):
        for plane in (0, 1):
            @pl.when(p.zh == plane)
            def _():
                attend(pair, plane + 1)
        step_b(jnp.int32(5 + pair))
        pol_step(jnp.int32(5 + pair))

    HALF = CW // 2

    def out_project(c):
        eb.ready(c)
        part[c] = (
            jnp.dot(att[p.zh], ol[c], preferred_element_type=F32)
            + jnp.dot(att[1 - p.zh], fr[c], preferred_element_type=F32)
        ).astype(BF)
        for d, dev in enumerate((p.xr, p.xl)):
            src = part.at[c, block(p.xo), pl.ds(d * HALF, HALF)]
            rcopy(src, r1.at[c, d], ssent, s1r.at[c], dev).start()

    def pass_on(c):
        rcopy(r1.at[c], r1.at[c], ssent, s1r.at[c], p.sib).wait_recv()
        for d, dev in enumerate((p.xr, p.xl)):
            rows, cols = block(p.xm if d else p.xp), pl.ds(d * HALF, HALF)
            part[c, rows, cols] = (part[c, rows, cols].astype(F32) + r1[c, d].astype(F32)).astype(BF)
            rcopy(part.at[c, rows], r2.at[c, d], ssent, s2r.at[c], dev).start()

    def finish(c):
        rcopy(r2.at[c], r2.at[c], ssent, s2r.at[c], p.sib).wait_recv()
        at = pl.ds(pl.multiple_of(c * CW, CW), CW)
        summed = part[c, own, :].astype(F32) + r2[c, 0].astype(F32) + r2[c, 1].astype(F32)
        out = (rv[c].astype(F32) + summed).astype(BF)
        hid[c] = out
        racc[...] = racc[...] + out.astype(F32) * head[at].astype(F32).reshape(1, CW)
        pltpu.make_async_copy(hid.at[c], hid_o.at[:, at], hsem).start()

    racc[...] = jnp.zeros_like(racc)

    @pl.loop(0, max(N + 2, 4 * LAG + 2))
    def _(it):
        step_b(it + 9)
        when_in(it, 0, N, out_project)
        when_in(it - 1, 0, N, pass_on)
        when_in(it - 2, 0, N, finish)
        pol_step(it + 9)

    @pl.when(p.core == 1)
    def _():
        for m in range(PCH):
            pol_arrived(m)

    store_pol = pltpu.make_async_copy(pol, pol_o, psem)
    store_pol.start()

    rows = jnp.sum(racc[...], axis=-1, keepdims=True)
    position = lax.broadcasted_iota(jnp.int32, (ROWS, 1), 0) + p.tp * ROWS
    picked = jnp.where(position == last - 1, 1.0, 0.0) + 512 ** (-0.5)
    share = jnp.sum(rows * picked, axis=0, keepdims=True)
    rsend[...] = jnp.broadcast_to(share, (8, 128))

    for t in range(8):
        @pl.when(t != p.tp)
        def _():
            rcopy(rsend, rrecv.at[p.tp], wsent, wrecv, (p.rep, t)).start()

        @pl.when(t == p.tp)
        def _():
            rrecv[t] = rsend[...]

    ea.drain()
    eb.drain()
    sent = tok.at[:, pl.ds(0, 3 * ROWS)]
    rcopy(sent, sent, tsent, tsent, p.sib).wait_send()
    sent = part.at[:, pl.ds(0, 3 * ROWS)]
    rcopy(sent, sent, ssent, ssent, p.sib).wait_send()
    pltpu.make_async_copy(hid, hid, hsem).wait()

    for target in targets:
        to, copy = kv_target(*target)

        @pl.when((to != p.tp) & (target[2] >= p.zh))
        def _():
            copy.wait_send()

    def pol_sent(way, start, size):
        ref = pol.at[pl.ds(start, size)]
        rcopy(ref, ref, psent.at[way], psem, p.sib).wait_send()

    @pl.when(first & ups)
    def _():
        pol_sent(0, 0, 4)

    @pl.when(first & downs)
    def _():
        pol_sent(1, 4, 4)

    @pl.when(first)
    def _():
        pol_sent(2, 0, PCH)

    @pl.when(p.core == 0)
    def _():
        pol_sent(3, 0, PCH)

    sent = rrecv.at[pl.ds(0, 7)]
    rcopy(sent, sent, wsent, wrecv, p.sib).wait()
    rew_o[0] = jnp.max(jnp.sum(rrecv[...], axis=0))
    store_pol.wait()


def on_device(residual_in, norm_gain, w_query, w_keyval, w_out, score_head, lengths, policy_slots):
    vmem = pl.BlockSpec(memory_space=pltpu.VMEM)
    smem = pl.BlockSpec(memory_space=pltpu.SMEM)
    hbm = pl.BlockSpec(memory_space=pl.ANY)
    dma = pltpu.SemaphoreType.DMA

    exchange_sems = [dma] + [dma((N,))] * 6
    prow = policy_slots.shape[1]
    hidden, reward, policy = pl.pallas_call(
        kernel,
        out_shape=(
            jax.ShapeDtypeStruct((ROWS, D), BF),
            jax.ShapeDtypeStruct((1,), F32),
            jax.ShapeDtypeStruct((PCH, prow // PCH, 1024), BF),
        ),
        in_specs=[vmem, vmem, smem, hbm, hbm, hbm, hbm, hbm],
        out_specs=(hbm, smem, hbm),
        scratch_shapes=[
            pltpu.VMEM((N, ROWS, CW), BF),
            pltpu.VMEM((N, PLANE, CW), BF),
            pltpu.VMEM((N, CW, WC), BF),
            pltpu.VMEM((N, CW, WC), BF),
            pltpu.VMEM((N, 512, CW), BF),
            pltpu.VMEM((N, 512, CW), BF),
            pltpu.VMEM((2, PLANE, WC), F32),
            pltpu.VMEM((2, PLANE, QC), BF),
            pltpu.VMEM((2, PLANE, HS), BF),
            pltpu.VMEM((2, 2, 2 * PLANE, HS), BF),
            pltpu.VMEM((2, PLANE, QC), BF),
            pltpu.VMEM((N, PLANE, CW), BF),
            pltpu.VMEM((N, 2, ROWS, CW // 2), BF),
            pltpu.VMEM((N, 2, ROWS, CW), BF),
            pltpu.VMEM((N, ROWS, CW), BF),
            pltpu.VMEM((ROWS, CW), F32),
            pltpu.VMEM((8, 128), F32),
            pltpu.VMEM((8, 8, 128), F32),
            pltpu.VMEM((PCH, prow // PCH, 1024), BF),
            dma, dma((N,)), dma, dma, dma((N,)), dma((N,)),
            *exchange_sems,
            *exchange_sems,
            dma((2, 4)), dma((2, 4)), dma, dma((N,)), dma((N,)),
            dma, dma, dma, dma((4,)), dma((PCH,)), dma,
        ],
        compiler_params=pltpu.CompilerParams(
            collective_id=0, has_side_effects=True, vmem_limit_bytes=66_000_000
        ),
        name="block",
    )(
        norm_gain, score_head, lengths,
        residual_in[0], w_query, w_keyval, w_out, policy_slots[0].reshape(PCH, prow // PCH, 1024),
    )
    return hidden[None], reward, policy.reshape(1, prow, 1024)


def solution(mesh):
    placed = (
        P("rep", "tp", None),
        P(),
        P(None, "tp"),
        P(None, "tp"),
        P("tp", None),
        P(),
        P("rep"),
        P("rep", None, "tp"),
    )
    return jax.shard_map(
        on_device,
        mesh=mesh,
        in_specs=placed,
        out_specs=(P("rep", "tp", None), P("rep"), P("rep", None, "tp")),
        check_vma=False,
    )
```

time: 152 us -> 192 us (1.26); the launches traced: 152 us -> 189 us
  Pallas kernels: 143 us -> 182 us
  local copies, waits for them, and re-layouts: 7.42 us -> 3.53 us
    pallas_call x1, Pallas kernels: 143 us -> 182 us  [on_device(): pl.pallas_call(kernel, out_shape=(jax.ShapeDtypeStruct((ROWS, D), BF), ja...]
    reshape x2 -> x0, local copies, waits for them, and re-layouts: 2.7 us -> none  [the longest x1 1.35 us: on_device(): norm_gain.reshape(1, D)]
where the time goes in v2:
time: 192 us; the launch traced here: 189 us
  Pallas kernels  182 us (95%)
  local copies, waits for them, and re-layouts  3.53 us (2%)
  between operations  3 us (2%)
    pallas_call x1, Pallas kernels, on_device(): pl.pallas_call(kernel, out_shape=(jax.ShapeDtypeStruct((ROWS, D), BF), ja...  182 us

profile of v2, /device:TPU:32, one launch (start us, length us, event | category | flops | bytes accessed | tf_op | source)
XLA Modules:
  0.0 188.7 jit_solution(13209738661074013798)
XLA Ops:
  1.3 182.2 %block.1 = (bf16[64,8192]{1,0:T(8,128)(2,1)}, f32[1]{0:T(128)}, bf16[8,96,1024]{2,1,0:T(8,128)(2,1)}) custom-call(bf16[8192]{0:T(1024)(128)(2,1)} %gain.1, bf16[8192]{0:T(1024)(128)(2,1)} %head.1, s32[1]{0:T(128)S(6)} %copy.14.length, bf16[64,8192]{1,0:T(8,128)(2,1)} %bitcast.6, bf16[8192,512]{1,0:T(8,128)(2,1)} %wq_h.1, bf16[8192,128]{1,0:T(8,128)(2,1)} %wkv_h.1, ...), custom_call_target="tpu_custom_call" | custom-call | tf_op jit(solution)/shard_map/block/pallas_call | solution.py:453
  183.4 0.0 copy-start
  183.5 2.4 %copy.15 = bf16[1,64,8192]{2,1,0:T(8,128)(2,1)} copy(bf16[1,64,8192]{2,1,0:T(8,128)(2,1)} %bitcast.7) | data formatting | bytes 2097152
  186.4 0.0 copy-done
  186.4 1.1 copy.17
Async XLA Ops:
  183.4 3.0 %copy-start = (bf16[8,96,1024]{2,1,0:T(8,128)(2,1)S(1)}, bf16[8,96,1024]{2,1,0:T(8,128)(2,1)}, u32[]{:S(2)}) copy-start(bf16[8,96,1024]{2,1,0:T(8,128)(2,1)} %get-tuple-element.8) | copy-start | bytes 4718596

commit v3 on v2

--- a/solution.py
+++ b/solution.py
@@ -14,9 +14,18 @@
 ROWS = 64
 PLANE = 256
 QC = 512
-WC = QC + 128
-PCH = 8
-LAG = 3
+KC = 128
+PCH = 16
+NK = 4
+E1, E2, E3, EP = 3, 6, 9, 11
+KV0, Q0, O0 = 0, NK, NK + N
+STEPS = O0 + N
+AHEAD = 4
+GAP = O0 + EP
+RL = 3
+POL = GAP + 1
+LAG = 2
+WG = 4
 MESH = pl.DeviceIdType.MESH
 BF = jnp.bfloat16
 F32 = jnp.float32
@@ -56,9 +65,10 @@
 
 
 class Exchange:
-    def __init__(self, p, near, far, rows, sems):
-        self.p, self.near, self.far, self.rows = p, near, far, rows
-        self.sent, self.cr, self.y1r, self.y2r, self.z1r, self.z2r, self.dr = sems
+    def __init__(self, p, near, far, base, sems):
+        self.p, self.near, self.far, self.base = p, near, far, base
+        self.count, self.rows = far.shape[:2]
+        self.sent, self.cr, self.y1r, self.y2r, self.z2r, self.dr = sems
 
     def piece(self, yy, core, sub=0, subs=4):
         size = self.rows // 32
@@ -67,16 +77,18 @@
 
     def move(self, k, where, rsem, dev):
         ref = self.far.at[k, where]
-        rcopy(ref, ref, self.sent, rsem.at[k], dev).start()
+        rcopy(ref, ref, self.sent, rsem.at[self.base + k], dev).start()
 
     def arrived(self, k, count, rsem):
         ref = self.far.at[k, pl.ds(0, count * (self.rows // 32))]
-        rcopy(ref, ref, self.sent, rsem.at[k], self.p.sib).wait_recv()
+        rcopy(ref, ref, self.sent, rsem.at[self.base + k], self.p.sib).wait_recv()
 
     def over_z(self, k):
         p = self.p
         where = self.piece(p.y, p.core)
-        rcopy(self.near.at[k, where], self.far.at[k, where], self.sent, self.cr.at[k], p.cross).start()
+        rcopy(
+            self.near.at[k, where], self.far.at[k, where], self.sent, self.cr.at[self.base + k], p.cross
+        ).start()
 
     def stage0(self, k):
         p = self.p
@@ -90,14 +102,13 @@
         self.arrived(k, 6, self.y1r)
         self.move(k, self.piece(p.ym, p.core, 2 * p.zl, 1), self.y2r, p.yr)
         self.move(k, self.piece(p.yp, p.core, 2 * p.zl + 1, 1), self.y2r, p.yl)
-        self.move(k, self.piece(p.ym, p.core, 3 * p.zl, 1), self.z1r, p.zpart)
-        self.move(k, self.piece(p.yp, p.core, 3 * p.zl, 1), self.z1r, p.zpart)
+        self.move(k, self.piece(p.ym, p.core, 3 * p.zl, 1), self.y2r, p.zpart)
+        self.move(k, self.piece(p.yp, p.core, 3 * p.zl, 1), self.y2r, p.zpart)
 
     def stage2(self, k):
         p = self.p
-        self.arrived(k, 2, self.y2r)
+        self.arrived(k, 4, self.y2r)
         self.move(k, self.piece(p.yo, p.core, 2 * p.zl, 2), self.z2r, p.zpart)
-        self.arrived(k, 2, self.z1r)
         self.move(k, self.piece(p.ym, p.core), self.dr, p.sib)
         self.move(k, self.piece(p.yp, p.core), self.dr, p.sib)
 
@@ -109,6 +120,13 @@
     def ready(self, k):
         self.arrived(k, 16, self.dr)
 
+    def stages(self, i):
+        k = i - self.base
+        when_in(k - E3, 0, self.count, self.stage3)
+        when_in(k - E2, 0, self.count, self.stage2)
+        when_in(k - E1, 0, self.count, self.stage1)
+        when_in(k, 0, self.count, self.stage0)
+
     def drain(self):
         rcopy(self.far, self.far, self.sent, self.sent, self.p.sib).wait_send()
 
@@ -116,15 +134,16 @@
 def kernel(
     gain, head, length, resid_h, wq_h, wkv_h, wo_h, pol_h,
     hid_o, rew_o, pol_o,
-    rv, tok, wl, wr, ol, fr, acc, qv, kvs, kva, att, part, r1, r2, hid, racc, rsend, rrecv, pol,
-    lsem, wsem, osem, tsent, t1r, t2r,
-    asent, acr, ay1r, ay2r, az1r, az2r, adr,
-    bsent, bcr, by1r, by2r, bz1r, bz2r, bdr,
+    rv, tok, wkl, wkr, wql, wqr, wol, wor, kacc, qacc, qv, kvs, kva, att, part, r1, r2, hid, racc, rsend, rrecv, pol,
+    lsem, wksem, wqsem, wosem, tsent, t1r, t2r,
+    ksent, qsent, osent, cr, y1r, y2r, z2r, dr,
     ks, kr, ssent, s1r, s2r, hsem, wsent, wrecv, psent, pr, psem,
 ):
     p = Place()
-    ea = Exchange(p, wl, wr, CW, (asent, acr, ay1r, ay2r, az1r, az2r, adr))
-    eb = Exchange(p, ol, fr, QC, (bsent, bcr, by1r, by2r, bz1r, bz2r, bdr))
+    recvs = (cr, y1r, y2r, z2r, dr)
+    ek = Exchange(p, wkl, wkr, KV0, (ksent, *recvs))
+    eq = Exchange(p, wql, wqr, Q0, (qsent, *recvs))
+    eo = Exchange(p, wol, wor, O0, (osent, *recvs))
 
     barrier = pltpu.get_barrier_semaphore()
     for t in range(8):
@@ -139,16 +158,16 @@
     for k in range(N):
         pltpu.make_async_copy(resid_h.at[:, pl.ds(k * CW, CW)], rv.at[k], lsem).start()
 
+    load_wk = pltpu.make_async_copy(wkv_h, wkl, wksem)
+    load_wk.start()
+    for g in range(WG):
+        part_of = pl.ds(g * N // WG, N // WG)
+        pltpu.make_async_copy(wq_h.at[part_of], wql.at[part_of], wqsem.at[g]).start()
+
     @pl.loop(0, N)
     def _(k):
         at = pl.ds(pl.multiple_of(k * CW, CW), CW)
-        pltpu.make_async_copy(wq_h.at[at], wl.at[k, :, pl.ds(0, QC)], wsem.at[k]).start()
-        pltpu.make_async_copy(wkv_h.at[at], wl.at[k, :, pl.ds(QC, 128)], wsem.at[k]).start()
-
-    @pl.loop(0, N)
-    def _(k):
-        at = pl.ds(pl.multiple_of(k * CW, CW), CW)
-        pltpu.make_async_copy(wo_h.at[:, at], ol.at[k], osem).start()
+        pltpu.make_async_copy(wo_h.at[:, at], wol.at[k], wosem).start()
 
     load_pol = pltpu.make_async_copy(pol_h, pol, psem)
 
@@ -192,40 +211,50 @@
     for k in range(2):
         tokens_send(k)
 
-    @pl.loop(0, N)
-    def _(k):
-        pltpu.make_async_copy(wl.at[k], wl.at[k], wsem.at[k]).wait()
-        ea.over_z(k)
-
-    acc[...] = jnp.zeros_like(acc)
-
-    def project(k):
+    load_wk.wait()
+    for k in range(NK):
+        ek.over_z(k)
+    for g in range(WG):
+        part_of = pl.ds(g * N // WG, N // WG)
+        pltpu.make_async_copy(wq_h.at[part_of], wql.at[part_of], wqsem.at[g]).wait()
+
+        @pl.loop(g * N // WG, (g + 1) * N // WG)
+        def _(k):
+            eq.over_z(k)
+
+    kacc[...] = jnp.zeros_like(kacc)
+    qacc[...] = jnp.zeros_like(qacc)
+
+    def project_kv(k):
         token_arrived(k, ROWS, t2r)
-        ea.ready(k)
-        acc[p.zh] = acc[p.zh] + jnp.dot(tok[k], wl[k], preferred_element_type=F32)
-        acc[1 - p.zh] = acc[1 - p.zh] + jnp.dot(tok[k], wr[k], preferred_element_type=F32)
-
-    def step_b(j):
-        @pl.when(j == -3)
-        def _():
-            pltpu.make_async_copy(ol, ol, osem).wait()
-
-        when_in(j + 3, 0, N, eb.over_z)
-        when_in(j - 6, 0, N, eb.stage3)
-        when_in(j - 5, 0, N, eb.stage2)
-        when_in(j - 4, 0, N, eb.stage1)
-        when_in(j, 0, N, eb.stage0)
-
-    @pl.loop(0, N + 4)
-    def _(i):
-        when_in(i + 2, 0, N, tokens_send)
-        when_in(i - 1, 0, N, tokens_forward)
-        when_in(i - 3, 0, N, ea.stage3)
-        when_in(i - 2, 0, N, ea.stage2)
-        when_in(i - 1, 0, N, ea.stage1)
-        when_in(i, 0, N, ea.stage0)
-        step_b(i - N)
-        when_in(i - 4, 0, N, project)
+
+        @pl.when(lax.rem(k, N // NK) == 0)
+        def _():
+            ek.ready(k // (N // NK))
+
+        rows = pl.ds(pl.multiple_of(lax.rem(k, N // NK) * CW, CW), CW)
+        for shard, w in ((p.zh, wkl), (1 - p.zh, wkr)):
+            kacc[shard] = kacc[shard] + jnp.dot(
+                tok[k], w[k // (N // NK), rows, :], preferred_element_type=F32
+            )
+
+    def project_q(k):
+        eq.ready(k)
+        qacc[p.zh] = qacc[p.zh] + jnp.dot(tok[k], wql[k], preferred_element_type=F32)
+        qacc[1 - p.zh] = qacc[1 - p.zh] + jnp.dot(tok[k], wqr[k], preferred_element_type=F32)
+
+    def step(i):
+        @pl.when(i == O0 - AHEAD)
+        def _():
+            pltpu.make_async_copy(wol, wol, wosem).wait()
+
+        when_in(i - O0 + AHEAD, 0, N, eo.over_z)
+        for exchange in (ek, eq, eo):
+            exchange.stages(i)
+
+    def token_step(c):
+        when_in(c + 2, 0, N, tokens_send)
+        when_in(c, 0, N, tokens_forward)
 
     first = (p.zl == 0) & (p.core == 0)
     ups = p.y < 3
@@ -238,44 +267,39 @@
     def pol_arrived(m):
         rcopy(pol.at[m], pol.at[m], psem, pr.at[m], p.sib).wait_recv()
 
-    def pol_fan(m):
-        pol_move(2, m, p.zpart)
-        pol_move(3, m, p.sib)
-
     def pol_step(j):
-        @pl.when(root & (j == 4))
+        @pl.when(root & (j == POL))
         def _():
             load_pol.wait()
 
         for d in (0, 1):
-            t = j - 4 - LAG * hops[d]
-            m = t // 2
-
-            @pl.when(first & (t >= 0) & (t < 8) & (lax.rem(t, 2) == 0))
+            t = j - POL - LAG * hops[d]
+            m = PCH // 2 * d + t // 2
+
+            @pl.when(first & (t >= 0) & (t < PCH) & (lax.rem(t, 2) == d))
             def _():
                 @pl.when(p.y > 0)
                 def _():
-                    pol_arrived(4 * d + m)
+                    pol_arrived(m)
 
                 @pl.when(downs if d else ups)
                 def _():
-                    pol_move(d, 4 * d + m, p.yl if d else p.yr)
-
-                pol_fan(4 * d + m)
+                    pol_move(d, m, p.yl if d else p.yr)
+
+                pol_move(2, m, p.zpart)
+                pol_move(3, m, p.sib)
 
             t2 = t - LAG
-            m2 = t2 // 2
-
-            @pl.when((p.zl == 1) & (p.core == 0) & (t2 >= 0) & (t2 < 8) & (lax.rem(t2, 2) == 0))
+            m2 = PCH // 2 * d + t2 // 2
+
+            @pl.when((p.zl == 1) & (p.core == 0) & (t2 >= 0) & (t2 < PCH) & (lax.rem(t2, 2) == d))
             def _():
-                pol_arrived(4 * d + m2)
-                pol_move(3, 4 * d + m2, p.sib)
-
-    for kind in (0, 1):
-        kvs[kind] = acc[kind, :, QC:].astype(BF)
+                pol_arrived(m2)
+                pol_move(3, m2, p.sib)
+
     slot = p.x // 2
     here = pl.ds(pl.multiple_of(p.zh * PLANE, PLANE), PLANE)
-    targets = [(kind, xd, zd) for kind in (0, 1) for zd in (1, 0) for xd in (0, 1)]
+    targets = [(kind, xd, zd) for kind in (0, 1) for zd in (0, 1) for xd in (0, 1)]
 
     def kv_target(kind, xd, zd):
         to = zd * 4 + 2 * lax.rem(p.x, 2) + xd
@@ -284,21 +308,41 @@
             kr.at[kind, slot * 2 + p.zh], (p.rep, to),
         )
 
-    for target in targets:
-        to, copy = kv_target(*target)
-
-        @pl.when((to != p.tp) & (target[2] >= p.zh))
-        def _():
-            copy.start()
-
-        @pl.when(to == p.tp)
-        def _():
-            kva[target[0], slot, here, :] = kvs[target[0]]
+    def kv_send():
+        for kind in (0, 1):
+            kvs[kind] = kacc[kind].astype(BF)
+        for target in targets:
+            to, copy = kv_target(*target)
+
+            @pl.when((to != p.tp) & (target[2] >= p.zh))
+            def _():
+                copy.start()
+
+            @pl.when(to == p.tp)
+            def _():
+                kva[target[0], slot, here, :] = kvs[target[0]]
+
+    @pl.loop(0, GAP)
+    def _(i):
+        c, off = 2 * i // 3, lax.rem(2 * i, 3)
+
+        @pl.when(off != 2)
+        def _():
+            token_step(c)
+
+        step(i)
+
+        when_in(i - EP - 1, 0, N, project_kv)
+
+        @pl.when(i == EP + N)
+        def _():
+            kv_send()
+
+        when_in(i - Q0 - EP, 0, N, project_q)
 
     for s in (0, 1):
-        qv[s] = acc[s, :, :QC].astype(BF)
-    step_b(jnp.int32(4))
-    pol_step(jnp.int32(4))
+        qv[s] = qacc[s].astype(BF)
+    step(jnp.int32(GAP))
 
     def kv_arrived(kind, planes):
         for j in (0, 1):
@@ -337,16 +381,16 @@
             @pl.when(p.zh == plane)
             def _():
                 attend(pair, plane + 1)
-        step_b(jnp.int32(5 + pair))
-        pol_step(jnp.int32(5 + pair))
+        step(jnp.int32(GAP + 1 + pair))
+        pol_step(jnp.int32(GAP + 1 + pair))
 
     HALF = CW // 2
 
     def out_project(c):
-        eb.ready(c)
+        eo.ready(c)
         part[c] = (
-            jnp.dot(att[p.zh], ol[c], preferred_element_type=F32)
-            + jnp.dot(att[1 - p.zh], fr[c], preferred_element_type=F32)
+            jnp.dot(att[p.zh], wol[c], preferred_element_type=F32)
+            + jnp.dot(att[1 - p.zh], wor[c], preferred_element_type=F32)
         ).astype(BF)
         for d, dev in enumerate((p.xr, p.xl)):
             src = part.at[c, block(p.xo), pl.ds(d * HALF, HALF)]
@@ -370,13 +414,13 @@
 
     racc[...] = jnp.zeros_like(racc)
 
-    @pl.loop(0, max(N + 2, 4 * LAG + 2))
+    @pl.loop(0, max(N + 2 * RL, PCH + 4 * LAG - 4))
     def _(it):
-        step_b(it + 9)
+        when_in(it - RL, 0, N, pass_on)
+        step(it + GAP + 5)
         when_in(it, 0, N, out_project)
-        when_in(it - 1, 0, N, pass_on)
-        when_in(it - 2, 0, N, finish)
-        pol_step(it + 9)
+        when_in(it - 2 * RL, 0, N, finish)
+        pol_step(it + GAP + 5)
 
     @pl.when(p.core == 1)
     def _():
@@ -401,8 +445,8 @@
         def _():
             rrecv[t] = rsend[...]
 
-    ea.drain()
-    eb.drain()
+    for exchange in (ek, eq, eo):
+        exchange.drain()
     sent = tok.at[:, pl.ds(0, 3 * ROWS)]
     rcopy(sent, sent, tsent, tsent, p.sib).wait_send()
     sent = part.at[:, pl.ds(0, 3 * ROWS)]
@@ -422,11 +466,11 @@
 
     @pl.when(first & ups)
     def _():
-        pol_sent(0, 0, 4)
+        pol_sent(0, 0, PCH // 2)
 
     @pl.when(first & downs)
     def _():
-        pol_sent(1, 4, 4)
+        pol_sent(1, PCH // 2, PCH // 2)
 
     @pl.when(first)
     def _():
@@ -448,7 +492,6 @@
     hbm = pl.BlockSpec(memory_space=pl.ANY)
     dma = pltpu.SemaphoreType.DMA
 
-    exchange_sems = [dma] + [dma((N,))] * 6
     prow = policy_slots.shape[1]
     hidden, reward, policy = pl.pallas_call(
         kernel,
@@ -462,11 +505,14 @@
         scratch_shapes=[
             pltpu.VMEM((N, ROWS, CW), BF),
             pltpu.VMEM((N, PLANE, CW), BF),
-            pltpu.VMEM((N, CW, WC), BF),
-            pltpu.VMEM((N, CW, WC), BF),
-            pltpu.VMEM((N, 512, CW), BF),
-            pltpu.VMEM((N, 512, CW), BF),
-            pltpu.VMEM((2, PLANE, WC), F32),
+            pltpu.VMEM((NK, D // NK, KC), BF),
+            pltpu.VMEM((NK, D // NK, KC), BF),
+            pltpu.VMEM((N, CW, QC), BF),
+            pltpu.VMEM((N, CW, QC), BF),
+            pltpu.VMEM((N, QC, CW), BF),
+            pltpu.VMEM((N, QC, CW), BF),
+            pltpu.VMEM((2, PLANE, KC), F32),
+            pltpu.VMEM((2, PLANE, QC), F32),
             pltpu.VMEM((2, PLANE, QC), BF),
             pltpu.VMEM((2, PLANE, HS), BF),
             pltpu.VMEM((2, 2, 2 * PLANE, HS), BF),
@@ -479,9 +525,8 @@
             pltpu.VMEM((8, 128), F32),
             pltpu.VMEM((8, 8, 128), F32),
             pltpu.VMEM((PCH, prow // PCH, 1024), BF),
-            dma, dma((N,)), dma, dma, dma((N,)), dma((N,)),
-            *exchange_sems,
-            *exchange_sems,
+            dma, dma, dma((WG,)), dma, dma, dma((N,)), dma((N,)),
+            dma, dma, dma, *[dma((STEPS,))] * 5,
             dma((2, 4)), dma((2, 4)), dma, dma((N,)), dma((N,)),
             dma, dma, dma, dma((4,)), dma((PCH,)), dma,
         ],
@@ -491,7 +536,8 @@
         name="block",
     )(
         norm_gain, score_head, lengths,
-        residual_in[0], w_query, w_keyval, w_out, policy_slots[0].reshape(PCH, prow // PCH, 1024),
+        residual_in[0], w_query.reshape(N, CW, QC), w_keyval.reshape(NK, D // NK, KC), w_out,
+        policy_slots[0].reshape(PCH, prow // PCH, 1024),
     )
     return hidden[None], reward, policy.reshape(1, prow, 1024)
 

time: 192 us -> 123 us (0.64); the launches traced: 189 us -> 123 us
  Pallas kernels: 182 us -> 116 us
    pallas_call x1, Pallas kernels: 182 us -> 116 us  [on_device(): pl.pallas_call(kernel, out_shape=(jax.ShapeDtypeStruct((ROWS, D), BF), ja...]
where the time goes in v3:
time: 123 us
  Pallas kernels  116 us (94%)
  local copies, waits for them, and re-layouts  3.53 us (3%)
  between operations  3 us (2%)
    pallas_call x1, Pallas kernels, on_device(): pl.pallas_call(kernel, out_shape=(jax.ShapeDtypeStruct((ROWS, D), BF), ja...  116 us
    unnamed x4, local copies, waits for them, and re-layouts  3.53 us

profile of v3, /device:TPU:32, one launch (start us, length us, event | category | flops | bytes accessed | tf_op | source)
XLA Modules:
  0.0 122.5 jit_solution(14698678033105835570)
XLA Ops:
  1.3 116.0 %block.1 = (bf16[64,8192]{1,0:T(8,128)(2,1)}, f32[1]{0:T(128)}, bf16[16,48,1024]{2,1,0:T(8,128)(2,1)}) custom-call(bf16[8192]{0:T(1024)(128)(2,1)} %gain.1, bf16[8192]{0:T(1024)(128)(2,1)} %head.1, s32[1]{0:T(128)S(6)} %copy.14.length, bf16[64,8192]{1,0:T(8,128)(2,1)} %bitcast.10, bf16[16,512,512]{2,1,0:T(8,128)(2,1)} %bitcast.6, ...), custom_call_target="tpu_custom_call" | custom-call | tf_op jit(solution)/shard_map/block/pallas_call | solution.py:496
  117.3 0.0 copy-start
  117.3 2.4 %copy.15 = bf16[1,64,8192]{2,1,0:T(8,128)(2,1)} copy(bf16[1,64,8192]{2,1,0:T(8,128)(2,1)} %bitcast.11) | data formatting | bytes 2097152
  120.3 0.0 copy-done
  120.3 1.1 copy.17
Async XLA Ops:
  117.3 3.0 %copy-start = (bf16[16,48,1024]{2,1,0:T(8,128)(2,1)S(1)}, bf16[16,48,1024]{2,1,0:T(8,128)(2,1)}, u32[]{:S(2)}) copy-start(bf16[16,48,1024]{2,1,0:T(8,128)(2,1)} %get-tuple-element.8) | copy-start | bytes 4718596

commit v4 on v3

--- a/solution.py
+++ b/solution.py
@@ -17,13 +17,15 @@
 KC = 128
 PCH = 16
 NK = 4
-E1, E2, E3, EP = 3, 6, 9, 11
+E1, E2, E3, EP = 3, 6, 9, 10
 KV0, Q0, O0 = 0, NK, NK + N
-STEPS = O0 + N
 AHEAD = 4
-GAP = O0 + EP
+GAP = NK + N + EP
+SLOW = 1
+V0 = -(-(GAP - O0) // SLOW)
+LEAD = 3
 RL = 3
-POL = GAP + 1
+POL = 5
 LAG = 2
 WG = 4
 MESH = pl.DeviceIdType.MESH
@@ -65,8 +67,8 @@
 
 
 class Exchange:
-    def __init__(self, p, near, far, base, sems):
-        self.p, self.near, self.far, self.base = p, near, far, base
+    def __init__(self, p, near, far, first, base, sems):
+        self.p, self.near, self.far, self.first, self.base = p, near, far, first, base
         self.count, self.rows = far.shape[:2]
         self.sent, self.cr, self.y1r, self.y2r, self.z2r, self.dr = sems
 
@@ -121,7 +123,7 @@
         self.arrived(k, 16, self.dr)
 
     def stages(self, i):
-        k = i - self.base
+        k = i - self.first
         when_in(k - E3, 0, self.count, self.stage3)
         when_in(k - E2, 0, self.count, self.stage2)
         when_in(k - E1, 0, self.count, self.stage1)
@@ -141,9 +143,9 @@
 ):
     p = Place()
     recvs = (cr, y1r, y2r, z2r, dr)
-    ek = Exchange(p, wkl, wkr, KV0, (ksent, *recvs))
-    eq = Exchange(p, wql, wqr, Q0, (qsent, *recvs))
-    eo = Exchange(p, wol, wor, O0, (osent, *recvs))
+    ek = Exchange(p, wkl, wkr, KV0, 0, (ksent, *recvs))
+    eq = Exchange(p, wql, wqr, Q0, NK, (qsent, *recvs))
+    eo = Exchange(p, wol, wor, 0, NK + N, (osent, *recvs))
 
     barrier = pltpu.get_barrier_semaphore()
     for t in range(8):
@@ -160,6 +162,8 @@
 
     load_wk = pltpu.make_async_copy(wkv_h, wkl, wksem)
     load_wk.start()
+    own = pl.ds(pl.multiple_of(p.x * ROWS, ROWS), ROWS)
+    pltpu.make_async_copy(rv, rv, lsem).wait()
     for g in range(WG):
         part_of = pl.ds(g * N // WG, N // WG)
         pltpu.make_async_copy(wq_h.at[part_of], wql.at[part_of], wqsem.at[g]).start()
@@ -175,8 +179,6 @@
     def _():
         load_pol.start()
 
-    own = pl.ds(pl.multiple_of(p.x * ROWS, ROWS), ROWS)
-    pltpu.make_async_copy(rv, rv, lsem).wait()
     squares = jnp.zeros((ROWS, 1), F32)
     for k in range(N):
         r = rv[k].astype(F32)
@@ -208,7 +210,7 @@
         token_move(k, block(p.xm, 0, 32), t2r, p.xr)
         token_move(k, block(p.xp, 32, 32), t2r, p.xl)
 
-    for k in range(2):
+    for k in range(LEAD):
         tokens_send(k)
 
     load_wk.wait()
@@ -243,17 +245,12 @@
         qacc[p.zh] = qacc[p.zh] + jnp.dot(tok[k], wql[k], preferred_element_type=F32)
         qacc[1 - p.zh] = qacc[1 - p.zh] + jnp.dot(tok[k], wqr[k], preferred_element_type=F32)
 
-    def step(i):
-        @pl.when(i == O0 - AHEAD)
-        def _():
-            pltpu.make_async_copy(wol, wol, wosem).wait()
-
-        when_in(i - O0 + AHEAD, 0, N, eo.over_z)
-        for exchange in (ek, eq, eo):
-            exchange.stages(i)
+    def output_step(v):
+        when_in(v + AHEAD, AHEAD, N, eo.over_z)
+        eo.stages(v)
 
     def token_step(c):
-        when_in(c + 2, 0, N, tokens_send)
+        when_in(c + LEAD, 0, N, tokens_send)
         when_in(c, 0, N, tokens_forward)
 
     first = (p.zl == 0) & (p.core == 0)
@@ -274,9 +271,9 @@
 
         for d in (0, 1):
             t = j - POL - LAG * hops[d]
-            m = PCH // 2 * d + t // 2
-
-            @pl.when(first & (t >= 0) & (t < PCH) & (lax.rem(t, 2) == d))
+            m = PCH // 2 * d + t
+
+            @pl.when(first & (t >= 0) & (t < PCH // 2))
             def _():
                 @pl.when(p.y > 0)
                 def _():
@@ -290,37 +287,62 @@
                 pol_move(3, m, p.sib)
 
             t2 = t - LAG
-            m2 = PCH // 2 * d + t2 // 2
-
-            @pl.when((p.zl == 1) & (p.core == 0) & (t2 >= 0) & (t2 < PCH) & (lax.rem(t2, 2) == d))
+            m2 = PCH // 2 * d + t2
+
+            @pl.when((p.zl == 1) & (p.core == 0) & (t2 >= 0) & (t2 < PCH // 2))
             def _():
                 pol_arrived(m2)
                 pol_move(3, m2, p.sib)
 
     slot = p.x // 2
+    near = lax.rem(p.x, 2)
     here = pl.ds(pl.multiple_of(p.zh * PLANE, PLANE), PLANE)
-    targets = [(kind, xd, zd) for kind in (0, 1) for zd in (0, 1) for xd in (0, 1)]
-
-    def kv_target(kind, xd, zd):
-        to = zd * 4 + 2 * lax.rem(p.x, 2) + xd
+    pair0 = 2 * near
+    nearest = pair0 + slot
+
+    def kv_in_plane(kind, off):
+        to = p.zh * 4 + pair0 + off
         return to, rcopy(
-            kvs.at[kind], kva.at[kind, slot, here], ks.at[kind, 2 * zd + xd],
-            kr.at[kind, slot * 2 + p.zh], (p.rep, to),
+            kvs.at[kind], kva.at[kind, slot, here], ks.at[kind, off], kr.at[kind, slot * 2 + p.zh],
+            (p.rep, to),
         )
+
+    def kv_up(kind):
+        return rcopy(
+            kvs.at[kind], kva.at[kind, slot, here], ks.at[kind, 2], kr.at[kind, slot * 2],
+            (p.rep, 4 + nearest),
+        )
+
+    def kv_beside(kind):
+        ref = kva.at[kind, near, pl.ds(0, PLANE)]
+        return rcopy(
+            ref, ref, ks.at[kind, 2], kr.at[kind, near * 2], (p.rep, 4 + p.x + 1 - 2 * near)
+        )
+
+    def kv_wait(kind, j, pz):
+        ref = kva.at[kind, j, pl.ds(pz * PLANE, PLANE)]
+        rcopy(ref, ref, ks.at[0, 0], kr.at[kind, j * 2 + pz], p.sib).wait_recv()
 
     def kv_send():
         for kind in (0, 1):
             kvs[kind] = kacc[kind].astype(BF)
-        for target in targets:
-            to, copy = kv_target(*target)
-
-            @pl.when((to != p.tp) & (target[2] >= p.zh))
-            def _():
-                copy.start()
-
-            @pl.when(to == p.tp)
-            def _():
-                kva[target[0], slot, here, :] = kvs[target[0]]
+
+        @pl.when(p.zh == 0)
+        def _():
+            for kind in (0, 1):
+                kv_up(kind).start()
+
+        for kind in (0, 1):
+            for off in (0, 1):
+                to, copy = kv_in_plane(kind, off)
+
+                @pl.when(to != p.tp)
+                def _():
+                    copy.start()
+
+                @pl.when(to == p.tp)
+                def _():
+                    kva[kind, slot, here, :] = kvs[kind]
 
     @pl.loop(0, GAP)
     def _(i):
@@ -330,11 +352,21 @@
         def _():
             token_step(c)
 
-        step(i)
-
-        when_in(i - EP - 1, 0, N, project_kv)
-
-        @pl.when(i == EP + N)
+        @pl.when(i == O0 - AHEAD)
+        def _():
+            pltpu.make_async_copy(wol, wol, wosem).wait()
+
+        when_in(i - O0 + AHEAD, 0, AHEAD, eo.over_z)
+        ek.stages(i)
+        eq.stages(i)
+
+        @pl.when((i >= O0) & (lax.rem(i - O0, SLOW) == 0))
+        def _():
+            output_step((i - O0) // SLOW)
+
+        when_in(i - EP, 0, N, project_kv)
+
+        @pl.when(i == EP + N - 1)
         def _():
             kv_send()
 
@@ -342,47 +374,59 @@
 
     for s in (0, 1):
         qv[s] = qacc[s].astype(BF)
-    step(jnp.int32(GAP))
-
-    def kv_arrived(kind, planes):
-        for j in (0, 1):
-            for pz in range(planes):
-                @pl.when(pz * 4 + 2 * j + p.x // 2 != p.tp)
-                def _():
-                    ref = kva.at[kind, j, pl.ds(pz * PLANE, PLANE)]
-                    rcopy(ref, ref, ks.at[0, 0], kr.at[kind, j * 2 + pz], p.sib).wait_recv()
+
+    @pl.when(p.zh == 1)
+    def _():
+        for kind in (0, 1):
+            kv_wait(kind, near, 0)
+            kv_beside(kind).start()
+
+    def kv_arrived(kind, j, plane):
+        @pl.when(2 * j + p.x // 2 != p.x)
+        def _():
+            kv_wait(kind, j, plane)
+
+        if plane == 1:
+            @pl.when(j != near)
+            def _():
+                kv_wait(kind, j, 0)
 
     last = length[0]
 
-    def attend(pair, planes):
+    def attend(turn, planes):
         keys = planes * PLANE
         rowpos = lax.broadcasted_iota(jnp.int32, (PLANE, keys), 0) + (planes - 1) * PLANE
         colpos = lax.broadcasted_iota(jnp.int32, (PLANE, keys), 1)
         valid = (colpos <= rowpos) & (colpos < last)
-        if pair == 0:
-            kv_arrived(0, planes)
-        for half in (0, 1):
-            s, h = pair // 2, 2 * (pair % 2) + half
-            cols = slice(h * HS, (h + 1) * HS)
-            scores = lax.dot_general(
+        s = near if turn == 0 else 1 - near
+        heads = [slice(h * HS, (h + 1) * HS) for h in range(4)]
+        kv_arrived(0, s, planes - 1)
+        scores = [
+            lax.dot_general(
                 qv[s, :, cols], kva[0, s, :keys, :], (((1,), (1,)), ((), ())),
                 preferred_element_type=F32,
             )
-            scores = jnp.where(valid, scores, -1e30)
-            top = jnp.max(scores, axis=-1, keepdims=True)
-            weight = jnp.exp2((scores - top) * (HS ** (-0.5) * 1.4426950408889634))
-            probs = (weight * (1.0 / jnp.sum(weight, axis=-1, keepdims=True))).astype(BF)
-            if pair == 0 and half == 0:
-                kv_arrived(1, planes)
-            att[s, :, cols] = jnp.dot(probs, kva[1, s, :keys, :], preferred_element_type=F32).astype(BF)
-
-    for pair in range(4):
+            for cols in heads
+        ]
+        scores = [jnp.where(valid, one, -1e30) for one in scores]
+        tops = [jnp.max(one, axis=-1, keepdims=True) for one in scores]
+        weights = [
+            jnp.exp2((one - top) * (HS ** (-0.5) * 1.4426950408889634)) for one, top in zip(scores, tops)
+        ]
+        probs = [
+            (one * (1.0 / jnp.sum(one, axis=-1, keepdims=True))).astype(BF) for one in weights
+        ]
+        kv_arrived(1, s, planes - 1)
+        for cols, one in zip(heads, probs):
+            att[s, :, cols] = jnp.dot(one, kva[1, s, :keys, :], preferred_element_type=F32).astype(BF)
+
+    for turn in (0, 1):
         for plane in (0, 1):
             @pl.when(p.zh == plane)
             def _():
-                attend(pair, plane + 1)
-        step(jnp.int32(GAP + 1 + pair))
-        pol_step(jnp.int32(GAP + 1 + pair))
+                attend(turn, plane + 1)
+        if turn == 0:
+            output_step(jnp.int32(V0))
 
     HALF = CW // 2
 
@@ -414,13 +458,13 @@
 
     racc[...] = jnp.zeros_like(racc)
 
-    @pl.loop(0, max(N + 2 * RL, PCH + 4 * LAG - 4))
+    @pl.loop(0, max(N + 2 * RL, POL + PCH // 2 + 4 * LAG))
     def _(it):
         when_in(it - RL, 0, N, pass_on)
-        step(it + GAP + 5)
         when_in(it, 0, N, out_project)
+        output_step(it + V0 + 1)
         when_in(it - 2 * RL, 0, N, finish)
-        pol_step(it + GAP + 5)
+        pol_step(it)
 
     @pl.when(p.core == 1)
     def _():
@@ -453,12 +497,15 @@
     rcopy(sent, sent, ssent, ssent, p.sib).wait_send()
     pltpu.make_async_copy(hid, hid, hsem).wait()
 
-    for target in targets:
-        to, copy = kv_target(*target)
-
-        @pl.when((to != p.tp) & (target[2] >= p.zh))
-        def _():
-            copy.wait_send()
+    for kind in (0, 1):
+        for off in (0, 1):
+            to, copy = kv_in_plane(kind, off)
+
+            @pl.when(to != p.tp)
+            def _():
+                copy.wait_send()
+
+        kv_up(kind).wait_send()
 
     def pol_sent(way, start, size):
         ref = pol.at[pl.ds(start, size)]
@@ -484,6 +531,26 @@
     rcopy(sent, sent, wsent, wrecv, p.sib).wait()
     rew_o[0] = jnp.max(jnp.sum(rrecv[...], axis=0))
     store_pol.wait()
+
+
+def write_out(hid_i, pol_i, hid_o, pol_o, hbuf, pbuf, rsem, wsem):
+    parts = 4
+    copies = []
+    for j, (src, buf, dst) in enumerate(((hid_i, hbuf, hid_o), (pol_i, pbuf, pol_o))):
+        size = src.shape[0] // parts
+        for m in range(parts):
+            at, s = pl.ds(m * size, size), j * parts + m
+            copies.append((
+                pltpu.make_async_copy(src.at[at], buf.at[at], rsem.at[s]),
+                pltpu.make_async_copy(buf.at[at], dst.at[at], wsem.at[s]),
+            ))
+    for read, _ in copies:
+        read.start()
+    for read, write in copies:
+        read.wait()
+        write.start()
+    for _, write in copies:
+        write.wait()
 
 
 def on_device(residual_in, norm_gain, w_query, w_keyval, w_out, score_head, lengths, policy_slots):
@@ -526,8 +593,8 @@
             pltpu.VMEM((8, 8, 128), F32),
             pltpu.VMEM((PCH, prow // PCH, 1024), BF),
             dma, dma, dma((WG,)), dma, dma, dma((N,)), dma((N,)),
-            dma, dma, dma, *[dma((STEPS,))] * 5,
-            dma((2, 4)), dma((2, 4)), dma, dma((N,)), dma((N,)),
+            dma, dma, dma, *[dma((NK + 2 * N,))] * 5,
+            dma((2, 3)), dma((2, 4)), dma, dma((N,)), dma((N,)),
             dma, dma, dma, dma((4,)), dma((PCH,)), dma,
         ],
         compiler_params=pltpu.CompilerParams(
@@ -539,6 +606,17 @@
         residual_in[0], w_query.reshape(N, CW, QC), w_keyval.reshape(NK, D // NK, KC), w_out,
         policy_slots[0].reshape(PCH, prow // PCH, 1024),
     )
+    hidden, policy = pl.pallas_call(
+        write_out,
+        out_shape=(
+            jax.ShapeDtypeStruct(hidden.shape, BF),
+            jax.ShapeDtypeStruct(policy.shape, BF),
+        ),
+        in_specs=[hbm, hbm],
+        out_specs=(hbm, hbm),
+        scratch_shapes=[pltpu.VMEM(hidden.shape, BF), pltpu.VMEM(policy.shape, BF), dma((8,)), dma((8,))],
+        name="write_out",
+    )(hidden, policy)
     return hidden[None], reward, policy.reshape(1, prow, 1024)
 
 

time: 123 us -> 113 us (0.919)
  Pallas kernels: 116 us -> 110 us
  local copies, waits for them, and re-layouts: 3.53 us -> 0 us
    pallas_call x1, Pallas kernels: 116 us -> 107 us  [on_device(): pl.pallas_call(kernel, out_shape=(jax.ShapeDtypeStruct((ROWS, D), BF), ja...]
    unnamed x4 -> x0, local copies, waits for them, and re-layouts: 3.53 us -> none
    pallas_call x0 -> x1, Pallas kernels: none -> 2.59 us  [on_device(): pl.pallas_call(write_out, out_shape=(jax.ShapeDtypeStruct(hidden.shape, B...]
where the time goes in v4:
time: 113 us
  Pallas kernels  110 us (97%)
  between operations  2.98 us (3%)
    pallas_call x1, Pallas kernels, on_device(): pl.pallas_call(kernel, out_shape=(jax.ShapeDtypeStruct((ROWS, D), BF), ja...  107 us
    pallas_call x1, Pallas kernels, on_device(): pl.pallas_call(write_out, out_shape=(jax.ShapeDtypeStruct(hidden.shape, B...  2.59 us

profile of v4, /device:TPU:32, one launch (start us, length us, event | category | flops | bytes accessed | tf_op | source)
XLA Modules:
  0.0 113.0 jit_solution(11904260105894620923)
XLA Ops:
  1.3 107.5 %block.1 = (bf16[64,8192]{1,0:T(8,128)(2,1)}, f32[1]{0:T(128)}, bf16[16,48,1024]{2,1,0:T(8,128)(2,1)}) custom-call(bf16[8192]{0:T(1024)(128)(2,1)} %gain.1, bf16[8192]{0:T(1024)(128)(2,1)} %head.1, s32[1]{0:T(128)S(6)} %copy.12.length, bf16[64,8192]{1,0:T(8,128)(2,1)} %bitcast.9, bf16[16,512,512]{2,1,0:T(8,128)(2,1)} %bitcast.6, ...), custom_call_target="tpu_custom_call" | custom-call | tf_op jit(solution)/shard_map/block/pallas_call | solution.py:563
  108.8 2.6 %write_out.1 = (bf16[64,8192]{1,0:T(8,128)(2,1)}, bf16[16,48,1024]{2,1,0:T(8,128)(2,1)}) custom-call(bf16[64,8192]{1,0:T(8,128)(2,1)} %get-tuple-element.8.hid_i, bf16[16,48,1024]{2,1,0:T(8,128)(2,1)} %get-tuple-element.9.pol_i), custom_call_target="tpu_custom_call" | custom-call | tf_op jit(solution)/shard_map/write_out/pallas_call | solution.py:609

commit v5 on v4

--- a/solution.py
+++ b/solution.py
@@ -24,7 +24,7 @@
 SLOW = 1
 V0 = -(-(GAP - O0) // SLOW)
 LEAD = 3
-RL = 3
+RL, RF = 3, 4
 POL = 5
 LAG = 2
 WG = 4
@@ -458,12 +458,12 @@
 
     racc[...] = jnp.zeros_like(racc)
 
-    @pl.loop(0, max(N + 2 * RL, POL + PCH // 2 + 4 * LAG))
+    @pl.loop(0, max(N + RL + RF, POL + PCH // 2 + 4 * LAG))
     def _(it):
         when_in(it - RL, 0, N, pass_on)
         when_in(it, 0, N, out_project)
         output_step(it + V0 + 1)
-        when_in(it - 2 * RL, 0, N, finish)
+        when_in(it - RL - RF, 0, N, finish)
         pol_step(it)
 
     @pl.when(p.core == 1)
@@ -533,7 +533,7 @@
     store_pol.wait()
 
 
-def write_out(hid_i, pol_i, hid_o, pol_o, hbuf, pbuf, rsem, wsem):
+def write_out(hid_i, pol_i, rew_i, hid_o, pol_o, rew_o, hbuf, pbuf, rbuf, rsem, wsem):
     parts = 4
     copies = []
     for j, (src, buf, dst) in enumerate(((hid_i, hbuf, hid_o), (pol_i, pbuf, pol_o))):
@@ -544,6 +544,10 @@
                 pltpu.make_async_copy(src.at[at], buf.at[at], rsem.at[s]),
                 pltpu.make_async_copy(buf.at[at], dst.at[at], wsem.at[s]),
             ))
+    copies.append((
+        pltpu.make_async_copy(rew_i, rbuf, rsem.at[2 * parts]),
+        pltpu.make_async_copy(rbuf, rew_o, wsem.at[2 * parts]),
+    ))
     for read, _ in copies:
         read.start()
     for read, write in copies:
@@ -606,17 +610,21 @@
         residual_in[0], w_query.reshape(N, CW, QC), w_keyval.reshape(NK, D // NK, KC), w_out,
         policy_slots[0].reshape(PCH, prow // PCH, 1024),
     )
-    hidden, policy = pl.pallas_call(
+    hidden, policy, reward = pl.pallas_call(
         write_out,
         out_shape=(
             jax.ShapeDtypeStruct(hidden.shape, BF),
             jax.ShapeDtypeStruct(policy.shape, BF),
+            jax.ShapeDtypeStruct(reward.shape, F32),
         ),
-        in_specs=[hbm, hbm],
-        out_specs=(hbm, hbm),
-        scratch_shapes=[pltpu.VMEM(hidden.shape, BF), pltpu.VMEM(policy.shape, BF), dma((8,)), dma((8,))],
+        in_specs=[hbm, hbm, hbm],
+        out_specs=(hbm, hbm, hbm),
+        scratch_shapes=[
+            pltpu.VMEM(hidden.shape, BF), pltpu.VMEM(policy.shape, BF), pltpu.SMEM((1,), F32),
+            dma((9,)), dma((9,)),
+        ],
         name="write_out",
-    )(hidden, policy)
+    )(hidden, policy, reward)
     return hidden[None], reward, policy.reshape(1, prow, 1024)
 
 

time: 113 us -> 112 us (level)
  between operations: 2.98 us -> 1.29 us
where the time goes in v5:
time: 112 us
  Pallas kernels  111 us (99%)
  between operations  1.29 us (1%)
    pallas_call x1, Pallas kernels, on_device(): pl.pallas_call(kernel, out_shape=(jax.ShapeDtypeStruct((ROWS, D), BF), ja...  108 us
    pallas_call x1, Pallas kernels, on_device(): pl.pallas_call(write_out, out_shape=(jax.ShapeDtypeStruct(hidden.shape, B...  3.17 us

profile of v5, /device:TPU:32, one launch (start us, length us, event | category | flops | bytes accessed | tf_op | source)
XLA Modules:
  0.0 112.0 jit_solution(16840396612726902170)
XLA Ops:
  1.3 107.5 %block.1 = (bf16[64,8192]{1,0:T(8,128)(2,1)}, f32[1]{0:T(128)}, bf16[16,48,1024]{2,1,0:T(8,128)(2,1)}) custom-call(bf16[8192]{0:T(1024)(128)(2,1)} %gain.1, bf16[8192]{0:T(1024)(128)(2,1)} %head.1, s32[1]{0:T(128)S(6)} %copy.11.length, bf16[64,8192]{1,0:T(8,128)(2,1)} %bitcast.9, bf16[16,512,512]{2,1,0:T(8,128)(2,1)} %bitcast.6, ...), custom_call_target="tpu_custom_call" | custom-call | tf_op jit(solution)/shard_map/block/pallas_call | solution.py:567
  108.8 3.2 %write_out.1 = (bf16[64,8192]{1,0:T(8,128)(2,1)}, bf16[16,48,1024]{2,1,0:T(8,128)(2,1)}, f32[1]{0:T(128)}) custom-call(bf16[64,8192]{1,0:T(8,128)(2,1)} %get-tuple-element.9.hid_i, bf16[16,48,1024]{2,1,0:T(8,128)(2,1)} %get-tuple-element.10.pol_i, f32[1]{0:T(128)} %get-tuple-element.11.rew_i), custom_call_target="tpu_custom_call" | custom-call | tf_op jit(solution)/shard_map/write_out/pallas_call | solution.py:613

commit v6 on v5

--- a/solution.py
+++ b/solution.py
@@ -19,13 +19,13 @@
 NK = 4
 E1, E2, E3, EP = 3, 6, 9, 10
 KV0, Q0, O0 = 0, NK, NK + N
-AHEAD = 4
+AHEAD = 5
 GAP = NK + N + EP
 SLOW = 1
 V0 = -(-(GAP - O0) // SLOW)
 LEAD = 3
 RL, RF = 3, 4
-POL = 5
+POL = 6
 LAG = 2
 WG = 4
 MESH = pl.DeviceIdType.MESH

time: 112 us -> 112 us (level); the launches traced: 112 us -> 110 us
  Pallas kernels: 111 us -> 109 us
    pallas_call x1, Pallas kernels: 108 us -> 105 us  [on_device(): pl.pallas_call(kernel, out_shape=(jax.ShapeDtypeStruct((ROWS, D), BF), ja...]
where the time goes in v6:
time: 112 us; the launch traced here: 110 us
  Pallas kernels  109 us (97%)
  between operations  1.29 us (1%)
    pallas_call x1, Pallas kernels, on_device(): pl.pallas_call(kernel, out_shape=(jax.ShapeDtypeStruct((ROWS, D), BF), ja...  105 us
    pallas_call x1, Pallas kernels, on_device(): pl.pallas_call(write_out, out_shape=(jax.ShapeDtypeStruct(hidden.shape, B...  3.17 us

profile of v6, /device:TPU:32, one launch (start us, length us, event | category | flops | bytes accessed | tf_op | source)
XLA Modules:
  0.0 109.8 jit_solution(2792129283688491745)
XLA Ops:
  1.3 105.4 %block.1 = (bf16[64,8192]{1,0:T(8,128)(2,1)}, f32[1]{0:T(128)}, bf16[16,48,1024]{2,1,0:T(8,128)(2,1)}) custom-call(bf16[8192]{0:T(1024)(128)(2,1)} %gain.1, bf16[8192]{0:T(1024)(128)(2,1)} %head.1, s32[1]{0:T(128)S(6)} %copy.11.length, bf16[64,8192]{1,0:T(8,128)(2,1)} %bitcast.9, bf16[16,512,512]{2,1,0:T(8,128)(2,1)} %bitcast.6, ...), custom_call_target="tpu_custom_call" | custom-call | tf_op jit(solution)/shard_map/block/pallas_call | solution.py:567
  106.7 3.2 %write_out.1 = (bf16[64,8192]{1,0:T(8,128)(2,1)}, bf16[16,48,1024]{2,1,0:T(8,128)(2,1)}, f32[1]{0:T(128)}) custom-call(bf16[64,8192]{1,0:T(8,128)(2,1)} %get-tuple-element.9.hid_i, bf16[16,48,1024]{2,1,0:T(8,128)(2,1)} %get-tuple-element.10.pol_i, f32[1]{0:T(128)} %get-tuple-element.11.rew_i), custom_call_target="tpu_custom_call" | custom-call | tf_op jit(solution)/shard_map/write_out/pallas_call | solution.py:613
